TPU v7x, 8 devices: a whole 2x2x1 slice. The times are simulated.
8 devices in a mesh: batch: 1 (over z), col: 2 (over y), row: 4 (over x, core).
Axes of the slice: x: 2, y: 2, z: 1, core: 2. Of those that a mesh axis runs over, the one named last changes fastest.
Arguments:
- a_matrix: float32 [16384, 64, 64], P(('batch', 'row'), 'col')
- b_matrix: float32 [16384, 64, 64], P(('batch', 'row'), 'col')
Outputs:
- output 1: float32 [16384, 64, 64], P(('batch', 'row'), 'col')
- output 2: float32 [256], P('batch')
- output 3: float32 [4, 64, 64], P('batch')
- output 4: float32 [16384, 64, 64], P(('batch', 'row'), 'col')
- output 5: float32 [256], P('batch')
- output 6: float32 [4, 64, 64], P('batch')
All inputs are finite; a program needn't handle non-finite values.
Results may differ from a plain program's by a relative error of at most 0.001.
Values sent between devices are 32-bit elements.
A program may use at most 1 GiB of HBM per device.

v0:
```python
import jax
import jax.numpy as jnp
from jax import lax
from jax.sharding import PartitionSpec as P

PANELS = 4
PRECISE = lax.Precision.HIGHEST


def factor_panel(panel_in, row_start, row_ids):
    panel_width = panel_in.shape[1]
    col_ids = jnp.arange(panel_width)

    def column_step(col_idx, loop_state):
        panel_work, tau_vec = loop_state
        diag_idx = row_start + col_idx
        column = lax.dynamic_slice_in_dim(panel_work, col_idx, 1, axis=1)[:, 0]
        below_diag = jnp.where(row_ids >= diag_idx, column, 0.0)
        at_diag = (row_ids == diag_idx).astype(jnp.float32)
        part_sums = jnp.stack([
            jnp.dot(below_diag, panel_work, precision=PRECISE, preferred_element_type=jnp.float32),
            jnp.dot(at_diag, panel_work, precision=PRECISE, preferred_element_type=jnp.float32)])
        summed = lax.psum(part_sums, "row")
        cross_vec = summed[0]
        diag_row = summed[1]
        pivot_val = lax.dynamic_slice_in_dim(diag_row, col_idx, 1)[0]
        col_norm = jnp.sqrt(lax.dynamic_slice_in_dim(cross_vec, col_idx, 1)[0])
        house_beta = -jnp.where(pivot_val >= 0, 1.0, -1.0) * col_norm
        house_tau = (house_beta - pivot_val) / house_beta
        denom_val = pivot_val - house_beta
        proj_row = jnp.where(col_ids > col_idx, (cross_vec - house_beta * diag_row) / denom_val, 0.0)
        refl_vec = jnp.where(row_ids > diag_idx, column / denom_val, 0.0) + at_diag
        panel_work = panel_work - house_tau * refl_vec[:, None] * proj_row[None, :]
        new_col = jnp.where(row_ids < diag_idx, column, jnp.where(row_ids == diag_idx, house_beta, refl_vec))
        panel_work = lax.dynamic_update_slice_in_dim(panel_work, new_col[:, None], col_idx, axis=1)
        tau_vec = lax.dynamic_update_slice_in_dim(tau_vec, house_tau[None], col_idx, axis=0)
        return panel_work, tau_vec

    return lax.fori_loop(0, panel_width, column_step, (panel_in, jnp.zeros((panel_width,), jnp.float32)))


def build_factor(gram_mat, tau_vec):
    panel_width = tau_vec.shape[0]
    col_ids = jnp.arange(panel_width)

    def t_step(col_idx, t_factor):
        gram_col = lax.dynamic_slice_in_dim(gram_mat, col_idx, 1, axis=1)[:, 0]
        gram_col = jnp.where(col_ids < col_idx, gram_col, 0.0)
        tau_k = lax.dynamic_slice_in_dim(tau_vec, col_idx, 1)[0]
        t_col = -tau_k * jnp.dot(t_factor, gram_col, precision=PRECISE, preferred_element_type=jnp.float32)
        t_col = jnp.where(col_ids == col_idx, tau_k, t_col)
        return lax.dynamic_update_slice_in_dim(t_factor, t_col[:, None], col_idx, axis=1)

    return lax.fori_loop(0, panel_width, t_step, jnp.zeros((panel_width, panel_width), jnp.float32))


def solution(mesh):
    col_procs = mesh.shape["col"]

    def factor_local(stored):
        local_rows, local_blocks, panel_width = stored.shape
        row_rank = lax.axis_index("row")
        col_rank = lax.axis_index("col")
        row_ids = row_rank * local_rows + jnp.arange(local_rows)
        col_ids = jnp.arange(panel_width)[None, :]
        tau_parts = []
        t_factors = []
        for panel_idx in range(PANELS):
            row_start = panel_idx * panel_width
            local_idx = panel_idx // col_procs
            is_owner = col_rank == panel_idx % col_procs
            panel_work, tau_vec = factor_panel(stored[:, local_idx, :], row_start, row_ids)
            diag_ids = row_start + col_ids
            v_block = jnp.where(row_ids[:, None] == diag_ids, 1.0, jnp.where(row_ids[:, None] > diag_ids, panel_work, 0.0))
            gram_mat = lax.psum(jnp.einsum("ri,rj->ij", v_block, v_block, precision=PRECISE, preferred_element_type=jnp.float32), "row")
            t_factor = build_factor(gram_mat, tau_vec)
            v_block, t_factor = lax.psum((jnp.where(is_owner, v_block, 0.0), jnp.where(is_owner, t_factor, 0.0)), "col")
            trailing = stored[:, local_idx:, :]
            proj_sum = lax.psum(jnp.einsum("ri,rbk->ibk", v_block, trailing, precision=PRECISE, preferred_element_type=jnp.float32), "row")
            w_block = jnp.einsum("ij,ibk->jbk", t_factor, proj_sum, precision=PRECISE, preferred_element_type=jnp.float32)
            updated = trailing - jnp.einsum("ri,ibk->rbk", v_block, w_block, precision=PRECISE, preferred_element_type=jnp.float32)
            block_ids = jnp.arange(local_blocks - local_idx)
            keep_mask = ((local_idx + block_ids) * col_procs + col_rank > panel_idx)[None, :, None]
            is_panel = ((block_ids == 0) & is_owner)[None, :, None]
            trailing = jnp.where(keep_mask, updated, jnp.where(is_panel, panel_work[:, None, :], trailing))
            stored = lax.dynamic_update_slice_in_dim(stored, trailing, local_idx, axis=1)
            tau_parts.append(jnp.diagonal(t_factor))
            t_factors.append(t_factor)
        return stored, jnp.concatenate(tau_parts), jnp.stack(t_factors)

    def factor_both(a_matrix, b_matrix):
        return factor_local(a_matrix) + factor_local(b_matrix)

    spec_mat = P(("batch", "row"), "col", None)
    spec_out = (spec_mat, P("batch"), P("batch", None, None))
    return jax.shard_map(factor_both, mesh=mesh, in_specs=(spec_mat, spec_mat), out_specs=spec_out + spec_out, check_vma=False)
```

profile of v0, /device:TPU:0, one launch (start us, length us, event | category | flops | bytes accessed | tf_op | source)
XLA Modules:
  0.0 8282.0 jit_solution(1913737647419551682)
XLA Ops:
  8.5 755.2 %while.252 = (s32[]{:T(128)}, f32[4096,64]{0,1:T(8,128)S(1)}, f32[64]{0:T(128)S(1)}, s32[]{:T(128)}, s32[]{:T(128)}, /*index=5*/f32[]{:T(128)}, f32[]{:T(128)}, f32[]{:T(128)}, s32[]{:T(128)}) while((s32[]{:T(128)}, f32[4096,64]{0,1:T(8,128)S(1)}, f32[64]{0:T(128)S(1)}, s32[]{:T(128)}, s32[]{:T(128)}, /*index=5*/f32[]{:T(128)}, ...), condition=%wide.region_38.39_spmd.clone, body=%wide.region_36.38_spmd.clone.sunk | while | flops 6877769 | bytes 4449039 | solution.py:39
  10.2 8.8 psum.364
  129.7 6.5 psum.364
  506.6 6.5 psum.364
  577.1 6.5 psum.364
  765.1 754.5 %while.248 = (s32[]{:T(128)}, f32[4096,64]{0,1:T(8,128)S(1)}, f32[64]{0:T(128)S(1)}, s32[]{:T(128)}, s32[]{:T(128)}, /*index=5*/f32[]{:T(128)}, f32[]{:T(128)}, f32[]{:T(128)}, s32[]{:T(128)}) while((s32[]{:T(128)}, f32[4096,64]{0,1:T(8,128)S(1)}, f32[64]{0:T(128)S(1)}, s32[]{:T(128)}, s32[]{:T(128)}, /*index=5*/f32[]{:T(128)}, ...), condition=%wide.region_2.3_spmd.clone, body=%wide.region_0.2_spmd.clone.sunk | while | flops 6877769 | bytes 4449039 | solution.py:39
  1250.0 6.5 psum.360
  1320.6 6.5 psum.360
  1523.5 11.5 all-reduce.3
  1535.1 132.0 %while.256 = (s32[]{:T(128)}, f32[64,64]{0,1:T(8,128)S(1)}, f32[64]{0:T(128)S(1)}, f32[64,64]{0,1:T(8,128)S(1)}, s32[]{:T(128)}, /*index=5*/s32[]{:T(128)}) while((s32[]{:T(128)}, f32[64,64]{0,1:T(8,128)S(1)}, f32[64]{0:T(128)S(1)}, f32[64,64]{0,1:T(8,128)S(1)}, s32[]{:T(128)}, /*index=5*/s32[]{:T(128)}) %tuple.585), condition=%wide.region_6.7_spmd.clone.clone, body=%wide.region_5.6_spmd.clone.clone.sunk | while | flops 49475 | bytes 36201 | solution.py:54
  1667.2 132.0 %while.260 = (s32[]{:T(128)}, f32[64,64]{0,1:T(8,128)S(1)}, f32[64]{0:T(128)S(1)}, f32[64,64]{0,1:T(8,128)S(1)}, s32[]{:T(128)}, /*index=5*/s32[]{:T(128)}) while((s32[]{:T(128)}, f32[64,64]{0,1:T(8,128)S(1)}, f32[64]{0:T(128)S(1)}, f32[64,64]{0,1:T(8,128)S(1)}, s32[]{:T(128)}, /*index=5*/s32[]{:T(128)}) %tuple.588), condition=%wide.region_42.43_spmd.clone.clone, body=%wide.region_41.42_spmd.clone.clone.sunk | while | flops 49475 | bytes 36201 | solution.py:54
  1799.5 8.0 all-reduce.11
  1811.8 52.2 fusion.208
  1865.6 52.5 fusion.201
  1921.9 44.6 all-reduce.31.cloned.1.call-done
  1970.0 31.4 fusion.342
  2003.6 30.6 fusion.338
  2034.2 65.0 select_select_fusion.1
  2100.5 764.4 %while.253 = (s32[]{:T(128)}, f32[4096,64]{0,1:T(8,128)S(1)}, f32[64]{0:T(128)S(1)}, s32[]{:T(128)}, s32[]{:T(128)}, /*index=5*/s32[]{:T(128)}, f32[]{:T(128)}, f32[]{:T(128)}, f32[]{:T(128)}, s32[]{:T(128)}) while((s32[]{:T(128)}, f32[4096,64]{0,1:T(8,128)S(1)}, f32[64]{0:T(128)S(1)}, s32[]{:T(128)}, s32[]{:T(128)}, ...), condition=%wide.region_47.48_spmd.clone, body=%wide.region_45.47_spmd.clone.sunk | while | flops 6877770 | bytes 4449059 | solution.py:39
  2221.3 6.5 psum.365
  2436.4 6.5 psum.365
  2651.5 6.5 psum.365
  2866.2 760.8 %while.249 = (s32[]{:T(128)}, f32[4096,64]{0,1:T(8,128)S(1)}, f32[64]{0:T(128)S(1)}, s32[]{:T(128)}, s32[]{:T(128)}, /*index=5*/s32[]{:T(128)}, f32[]{:T(128)}, f32[]{:T(128)}, f32[]{:T(128)}, s32[]{:T(128)}) while((s32[]{:T(128)}, f32[4096,64]{0,1:T(8,128)S(1)}, f32[64]{0:T(128)S(1)}, s32[]{:T(128)}, s32[]{:T(128)}, ...), condition=%wide.region_11.12_spmd.clone, body=%wide.region_9.11_spmd.clone.sunk | while | flops 6877770 | bytes 4449059 | solution.py:39
  2868.1 6.5 psum.361
  3082.0 6.5 psum.361
  3296.0 6.5 psum.361
  3509.9 6.5 psum.361
  3631.4 11.2 all-reduce.2
  3642.7 132.0 %while.257 = (s32[]{:T(128)}, f32[64,64]{0,1:T(8,128)S(1)}, f32[64]{0:T(128)S(1)}, f32[64,64]{0,1:T(8,128)S(1)}, s32[]{:T(128)}, /*index=5*/s32[]{:T(128)}) while((s32[]{:T(128)}, f32[64,64]{0,1:T(8,128)S(1)}, f32[64]{0:T(128)S(1)}, f32[64,64]{0,1:T(8,128)S(1)}, s32[]{:T(128)}, /*index=5*/s32[]{:T(128)}) %tuple.597), condition=%wide.region_15.16_spmd.clone.clone, body=%wide.region_14.15_spmd.clone.clone.sunk | while | flops 49475 | bytes 36201 | solution.py:54
  3774.9 52.2 fusion.206
  3828.7 52.6 fusion.199
  3882.9 132.0 %while.261 = (s32[]{:T(128)}, f32[64,64]{0,1:T(8,128)S(1)}, f32[64]{0:T(128)S(1)}, f32[64,64]{0,1:T(8,128)S(1)}, s32[]{:T(128)}, /*index=5*/s32[]{:T(128)}) while((s32[]{:T(128)}, f32[64,64]{0,1:T(8,128)S(1)}, f32[64]{0:T(128)S(1)}, f32[64,64]{0,1:T(8,128)S(1)}, s32[]{:T(128)}, /*index=5*/s32[]{:T(128)}) %tuple.600), condition=%wide.region_51.52_spmd.clone.clone, body=%wide.region_50.51_spmd.clone.clone.sunk | while | flops 49475 | bytes 36201 | solution.py:54
  4015.2 11.2 all-reduce.10
  4032.6 31.5 fusion.343
  4066.3 30.3 fusion.339
  4096.5 65.0 select_select_fusion
  4162.9 753.1 %while.254 = (s32[]{:T(128)}, f32[4096,64]{0,1:T(8,128)S(1)}, f32[64]{0:T(128)S(1)}, s32[]{:T(128)}, s32[]{:T(128)}, /*index=5*/s32[]{:T(128)}, f32[]{:T(128)}, f32[]{:T(128)}, f32[]{:T(128)}, s32[]{:T(128)}) while((s32[]{:T(128)}, f32[4096,64]{0,1:T(8,128)S(1)}, f32[64]{0:T(128)S(1)}, s32[]{:T(128)}, s32[]{:T(128)}, ...), condition=%wide.region_56.57_spmd.clone, body=%wide.region_54.56_spmd.clone.sunk | while | flops 6877770 | bytes 4449059 | solution.py:39
  4175.9 6.5 psum.366
  4223.0 6.5 psum.366
  4270.1 6.5 psum.366
  4317.1 6.5 psum.366
  4364.2 6.5 psum.366
  4917.3 753.2 %while.250 = (s32[]{:T(128)}, f32[4096,64]{0,1:T(8,128)S(1)}, f32[64]{0:T(128)S(1)}, s32[]{:T(128)}, s32[]{:T(128)}, /*index=5*/s32[]{:T(128)}, f32[]{:T(128)}, f32[]{:T(128)}, f32[]{:T(128)}, s32[]{:T(128)}) while((s32[]{:T(128)}, f32[4096,64]{0,1:T(8,128)S(1)}, f32[64]{0:T(128)S(1)}, s32[]{:T(128)}, s32[]{:T(128)}, ...), condition=%wide.region_20.21_spmd.clone, body=%wide.region_18.20_spmd.clone.sunk | while | flops 6877770 | bytes 4449059 | solution.py:39
  5674.8 10.7 all-reduce.1
  5685.7 121.2 %while.262 = (s32[]{:T(128)}, f32[64,64]{0,1:T(8,128)S(1)}, f32[64]{0:T(128)S(1)}, f32[64,64]{0,1:T(8,128)S(1)}, s32[]{:T(128)}, /*index=5*/s32[]{:T(128)}) while((s32[]{:T(128)}, f32[64,64]{0,1:T(8,128)S(1)}, f32[64]{0:T(128)S(1)}, f32[64,64]{0,1:T(8,128)S(1)}, s32[]{:T(128)}, /*index=5*/s32[]{:T(128)}) %tuple.609), condition=%wide.region_60.61_spmd.clone.clone, body=%wide.region_59.60_spmd.clone.clone.sunk | while | flops 49475 | bytes 36201 | solution.py:54
  5807.0 52.7 fusion.194
  5861.4 52.7 fusion.192
  5915.8 139.5 %while.258 = (s32[]{:T(128)}, f32[64,64]{0,1:T(8,128)S(1)}, f32[64]{0:T(128)S(1)}, f32[64,64]{0,1:T(8,128)S(1)}, s32[]{:T(128)}, /*index=5*/s32[]{:T(128)}) while((s32[]{:T(128)}, f32[64,64]{0,1:T(8,128)S(1)}, f32[64]{0:T(128)S(1)}, f32[64,64]{0,1:T(8,128)S(1)}, s32[]{:T(128)}, /*index=5*/s32[]{:T(128)}) %tuple.612), condition=%wide.region_24.25_spmd.clone.clone, body=%wide.region_23.24_spmd.clone.clone.sunk | while | flops 49475 | bytes 36201 | solution.py:54
  6055.5 7.6 all-reduce.9
  6068.2 30.1 fusion.344
  6100.5 29.7 fusion.340
  6130.2 86.1 %constant_dynamic-update-slice_fusion = (f32[4096,32,64]{0,2,1:T(8,128)}, f32[4096,31,64]{0,2,1:T(8,128)}, f32[4096,32,64]{0,2,1:T(8,128)}, f32[4096,31,64]{0,2,1:T(8,128)}) fusion(f32[4096,32,64]{0,2,1:T(8,128)} %get-tuple-element.2182, f32[4096,64]{0,1:T(8,128)S(1)} %get-tuple-element.1560, pred[31]{0:T(512)(128)(4,1)S(1)} %copy-done.30, ...), kind=kLoop, calls=%fused_computation.417 | loop fusion | flops 48758784 | bytes 262144064 | tf_op jit(solution)/shard_map/dynamic_update_slice | solution.py:86
  6217.6 753.3 %while.255 = (s32[]{:T(128)}, f32[4096,64]{0,1:T(8,128)S(1)}, f32[64]{0:T(128)S(1)}, s32[]{:T(128)}, s32[]{:T(128)}, /*index=5*/s32[]{:T(128)}, f32[]{:T(128)}, f32[]{:T(128)}, f32[]{:T(128)}, s32[]{:T(128)}) while((s32[]{:T(128)}, f32[4096,64]{0,1:T(8,128)S(1)}, f32[64]{0:T(128)S(1)}, s32[]{:T(128)}, s32[]{:T(128)}, ...), condition=%wide.region_65.66_spmd.clone, body=%wide.region_63.65_spmd.clone.sunk | while | flops 6877770 | bytes 4449059 | solution.py:39
  6972.2 753.5 %while.251 = (s32[]{:T(128)}, f32[4096,64]{0,1:T(8,128)S(1)}, f32[64]{0:T(128)S(1)}, s32[]{:T(128)}, s32[]{:T(128)}, /*index=5*/s32[]{:T(128)}, f32[]{:T(128)}, f32[]{:T(128)}, f32[]{:T(128)}, s32[]{:T(128)}) while((s32[]{:T(128)}, f32[4096,64]{0,1:T(8,128)S(1)}, f32[64]{0:T(128)S(1)}, s32[]{:T(128)}, s32[]{:T(128)}, ...), condition=%wide.region_29.30_spmd.clone, body=%wide.region_27.29_spmd.clone.sunk | while | flops 6877770 | bytes 4449059 | solution.py:39
  7730.0 10.7 all-reduce
  7740.8 132.0 %while.259 = (s32[]{:T(128)}, f32[64,64]{0,1:T(8,128)S(1)}, f32[64]{0:T(128)S(1)}, f32[64,64]{0,1:T(8,128)S(1)}, s32[]{:T(128)}, /*index=5*/s32[]{:T(128)}) while((s32[]{:T(128)}, f32[64,64]{0,1:T(8,128)S(1)}, f32[64]{0:T(128)S(1)}, f32[64,64]{0,1:T(8,128)S(1)}, s32[]{:T(128)}, /*index=5*/s32[]{:T(128)}) %tuple.621), condition=%wide.region_33.34_spmd.clone.clone, body=%wide.region_32.33_spmd.clone.clone.sunk | while | flops 49475 | bytes 36201 | solution.py:54
  7873.0 132.0 %while.263 = (s32[]{:T(128)}, f32[64,64]{0,1:T(8,128)S(1)}, f32[64]{0:T(128)S(1)}, f32[64,64]{0,1:T(8,128)S(1)}, s32[]{:T(128)}, /*index=5*/s32[]{:T(128)}) while((s32[]{:T(128)}, f32[64,64]{0,1:T(8,128)S(1)}, f32[64]{0:T(128)S(1)}, f32[64,64]{0,1:T(8,128)S(1)}, s32[]{:T(128)}, /*index=5*/s32[]{:T(128)}) %tuple.624), condition=%wide.region_69.70_spmd.clone.clone, body=%wide.region_68.69_spmd.clone.clone.sunk | while | flops 49475 | bytes 36201 | solution.py:54
  8005.3 45.1 fusion.203
  8052.0 45.1 fusion.196
  8098.8 9.9 all-reduce.8
  8112.9 33.0 all-reduce.25.cloned.1.call-done
  8149.4 30.6 fusion.345
  8182.1 29.4 fusion.341
  8211.4 63.5 select_dynamic-update-slice_fusion
  (10410 shorter events, 5344.7 us)
Async XLA Ops:
  7.2 1804.6 %all-reduce.39.cloned.1.call-start = ((), (), s32[]{:S(2)}) async-start(), calls=%async_computation.7 | async-start | bytes 4194304 | tf_op jit(solution)/shard_map/psum | solution.py:77
  1521.2 445.2 %all-reduce.31.cloned.1.call-start = ((), (), s32[]{:S(2)}) async-start(), calls=%async_computation.3 | async-start | bytes 4194304 | tf_op jit(solution)/shard_map/psum | solution.py:79
  1807.4 159.1 %copy-start.2 = (f32[64,64]{1,0:T(8,128)}, f32[64,64]{1,0:T(8,128)S(1)}, u32[]{:S(2)}) copy-start(f32[64,64]{1,0:T(8,128)S(1)} %get-tuple-element.2093) | copy-start | bytes 49156
  1807.5 193.9 %copy-start.4 = (f32[64,64]{1,0:T(8,128)}, f32[64,64]{1,0:T(8,128)S(1)}, u32[]{:S(2)}) copy-start(f32[64,64]{1,0:T(8,128)S(1)} %get-tuple-element.2092) | copy-start | bytes 49156
  1807.5 110.6 %copy-start = (s32[64]{0:T(128)}, s32[64]{0:T(128)S(1)}, u32[]{:S(2)}) copy-start(s32[64]{0:T(128)S(1)} %or_bitcast_fusion) | copy-start | bytes 772
  1811.8 53.8 copy-start.15
  1918.1 85.4 %copy-start.14 = (f32[4096,64]{0,1:T(8,128)S(1)}, f32[4096,64]{0,1:T(8,128)}, u32[]{:S(2)}) copy-start(f32[4096,64]{0,1:T(8,128)} %get-tuple-element.2100) | copy-start | bytes 3145732
  1919.7 1855.1 %all-reduce.37.cloned.1.call-start = ((), (), s32[]{:S(2)}) async-start(), calls=%async_computation.6 | async-start | bytes 4194304 | tf_op jit(solution)/shard_map/psum | solution.py:77
  1966.5 34.9 copy-start.19
  3642.7 386.4 %all-reduce.29.cloned.1.call-start = ((), (), s32[]{:S(2)}) async-start(), calls=%async_computation.2 | async-start | bytes 4194304 | tf_op jit(solution)/shard_map/psum | solution.py:79
  3774.9 53.8 copy-start.17
  3827.1 199.4 %copy-start.1 = (s32[64]{0:T(128)S(1)}, s32[64]{0:T(128)}, u32[]{:S(2)}) copy-start(s32[64]{0:T(128)} %copy-done) | copy-start | bytes 772
  3881.3 185.0 %copy-start.16 = (f32[4096,64]{0,1:T(8,128)S(1)}, f32[4096,64]{0,1:T(8,128)}, u32[]{:S(2)}) copy-start(f32[4096,64]{0,1:T(8,128)} %get-tuple-element.2098) | copy-start | bytes 3145732
  3882.9 1924.1 %all-reduce.35.cloned.1.call-start = ((), (), s32[]{:S(2)}) async-start(), calls=%async_computation.5 | async-start | bytes 4194304 | tf_op jit(solution)/shard_map/psum | solution.py:77
  4026.4 70.1 copy-start.6
  4026.4 70.1 copy-start.8
  4029.1 35.0 copy-start.18
  4032.6 63.9 copy-start.32
  4161.6 1508.9 %copy-start.27 = (s32[64]{0:T(128)S(1)}, s32[64]{0:T(128)}, u32[]{:S(2)}) copy-start(s32[64]{0:T(128)} %iota_add_fusion.10) | copy-start | bytes 772
  5685.6 379.1 %all-reduce.27.cloned.1.call-start = ((), (), s32[]{:S(2)}) async-start(), calls=%async_computation.1 | async-start | bytes 4194304 | tf_op jit(solution)/shard_map/psum | solution.py:79
  5807.0 54.4 copy-start.11
  5914.1 186.4 %copy-start.10 = (f32[4096,64]{0,1:T(8,128)S(1)}, f32[4096,64]{0,1:T(8,128)}, u32[]{:S(2)}) copy-start(f32[4096,64]{0,1:T(8,128)} %get-tuple-element.2096) | copy-start | bytes 3145732
  5915.8 2089.5 %all-reduce.33.cloned.1.call-start = ((), (), s32[]{:S(2)}) async-start(), calls=%async_computation.4 | async-start | bytes 4194304 | tf_op jit(solution)/shard_map/psum | solution.py:77
  6064.7 33.6 copy-start.20
  6068.2 62.0 copy-start.30
  6068.2 62.0 copy-start.31
  6216.3 1509.5 %copy-start.26 = (s32[64]{0:T(128)S(1)}, s32[64]{0:T(128)}, u32[]{:S(2)}) copy-start(s32[64]{0:T(128)} %iota_add_fusion.9) | copy-start | bytes 772
  7873.0 272.9 %all-reduce.25.cloned.1.call-start = ((), (), s32[]{:S(2)}) async-start(), calls=%async_computation | async-start | bytes 4194304 | tf_op jit(solution)/shard_map/psum | solution.py:79
  8005.3 46.8 copy-start.13
  8050.4 59.9 copy-start.23
  8050.4 59.9 copy-start.25
  8050.4 60.6 copy-start.22
  8050.4 60.6 copy-start.24
  8050.4 61.2 copy-start.5
  8050.4 61.2 copy-start.9
  8050.4 61.8 copy-start.3
  8050.5 61.8 copy-start.7
  8097.1 84.9 %copy-start.12 = (f32[4096,64]{0,1:T(8,128)S(1)}, f32[4096,64]{0,1:T(8,128)}, u32[]{:S(2)}) copy-start(f32[4096,64]{0,1:T(8,128)} %get-tuple-element.2094) | copy-start | bytes 3145732
  8145.9 34.0 copy-start.21
  8149.3 62.1 copy-start.28
  8149.4 62.1 copy-start.29
Sparse Core Ops, SparseCore 0:
  1521.4 56.4 all-reduce.38
  1919.8 46.6 all-reduce.30
  3642.8 59.8 all-reduce.36
  3883.0 48.3 all-reduce.28
  5685.8 56.8 all-reduce.34
  5915.9 45.3 all-reduce.26
  7873.1 58.4 all-reduce.32
  8098.9 46.9 all-reduce.24
where the time goes:
time: 8330 us; the launch traced here: 8280 us
  blocking collectives  3160 us (38%)
  matrix products  1850 us (22%)
  loops' own time  1720 us (21%)
  local copies, waits for them, and re-layouts  963 us (12%)
  other arithmetic  501 us (6%)
    psum x512, blocking collectives, column_step(): summed = lax.psum(part_sums, 'row')  3080 us
    another operation x8, loops' own time, factor_panel(): lax.fori_loop(0, panel_width, column_step, (panel_in, jnp.zeros((panel_wi...  1380 us
    dot_general x512, matrix products, column_step(): jnp.dot(below_diag, panel_work, precision=PRECISE, preferred_element_type...  469 us
    dot_general x8, matrix products, factor_local(): jnp.einsum('ri,rbk->ibk', v_block, trailing, precision=PRECISE, preferred...  405 us
    dot_general x512, matrix products, t_step(): jnp.dot(t_factor, gram_col, precision=PRECISE, preferred_element_type=jnp...  397 us
    another operation x8, loops' own time, build_factor(): lax.fori_loop(0, panel_width, t_step, jnp.zeros((panel_width, panel_width...  339 us
    dynamic_slice x512, local copies, waits for them, and re-layouts, column_step(): pivot_val = lax.dynamic_slice_in_dim(diag_row, col_idx, 1)[0]  323 us
    dynamic_slice x512, local copies, waits for them, and re-layouts, t_step(): tau_k = lax.dynamic_slice_in_dim(tau_vec, col_idx, 1)[0]  304 us

commit v1 on v0

v1 whole, which is shorter than its diff:
```python
import functools

import jax
import jax.numpy as jnp
from jax import lax
from jax.experimental import pallas as pl
from jax.experimental.pallas import tpu as pltpu
from jax.sharding import PartitionSpec as P

F32 = jnp.float32
BF = jnp.bfloat16
HI = lax.Precision.HIGHEST
PANELS = 4
W = 64
NP = 4
N = 256
NN = (((1,), (0,)), ((), ()))
NT = (((1,), (1,)), ((), ()))
TN = (((0,), (0,)), ((), ()))


BOTH = (0, 1)
TILE = (8, 128)


def rows_of(shape):
    return lax.broadcasted_iota(jnp.int32, shape, 0)


def lanes_of(shape):
    return lax.broadcasted_iota(jnp.int32, shape, 1)


def hdot(a, b, dn=NN):
    return lax.dot_general(a, b, dn, precision=HI, preferred_element_type=F32)


GROUP = 4
AMPLIFY = 64.0
HUGE = 1e9


def diag_factor(mats):
    tiles = W // 8
    lane8 = lanes_of(TILE)
    sub8 = rows_of(TILE)
    r64 = rows_of((W, W))
    c64 = lanes_of((W, W))
    eye = (r64 == c64).astype(F32)
    full = lambda x: jnp.broadcast_to(x, TILE)
    zeros = jnp.zeros(TILE, F32)
    st = []
    for hpp, ypp in mats:
        he = jnp.concatenate([hpp, eye], 1)
        yw = jnp.concatenate([ypp, eye], 1)
        st.append(dict(he=[he[8 * g:8 * g + 8] for g in range(tiles)], yw=[yw[8 * g:8 * g + 8] for g in range(tiles)],
                       l=[zeros] * tiles, u=[zeros] * tiles, tau=zeros))
    for k0 in range(0, W, GROUP):
        gk = k0 // 8
        for s in st:
            s['bh'] = [[full(s['he'][g][:, k:k + 1]) for g in range(gk, tiles)] for k in range(k0, k0 + GROUP)]
            s['by'] = [[full(s['yw'][g][:, k:k + 1]) for g in range(tiles)] for k in range(k0, k0 + GROUP)]
        for k in range(k0, k0 + GROUP):
            sk = k - 8 * gk
            isk = sub8 == sk
            for s in st:
                ch, cy = s['bh'][k - k0], s['by'][k - k0]
                pick = lambda x: full(x[sk:sk + 1, :])
                h = pick(ch[0])
                a = pick(cy[gk])
                rs = lax.rsqrt(h)
                rinv = jnp.where(a >= 0, -rs, rs)
                ukk = a - h * rinv
                uinv = 1.0 / ukk
                r = pick(s['he'][gk]) * rinv
                u = pick(s['yw'][gk]) - jnp.where((lane8 >= k) & (lane8 < W), r, 0.0)
                un = u * uinv
                rr = r * rinv
                for k2 in range(k + 1, k0 + GROUP):
                    r2 = pick(s['bh'][k2 - k0][0]) * rinv
                    un2 = (pick(s['by'][k2 - k0][gk]) - r2) * uinv
                    rr2 = r2 * rinv
                    s['bh'][k2 - k0] = [x - ch[i] * rr2 for i, x in enumerate(s['bh'][k2 - k0])]
                    nby = [x - cy[i] * un2 for i, x in enumerate(s['by'][k2 - k0])]
                    nby[gk] = jnp.where(isk, un2, nby[gk])
                    s['by'][k2 - k0] = nby
                for g in range(gk, tiles):
                    new = s['he'][g] - ch[g - gk] * rr
                    lc = cy[g] * uinv
                    if g == gk:
                        new = jnp.where(sub8 > sk, new, jnp.where(isk, r, s['he'][g]))
                        lc = jnp.where(sub8 > sk, lc, 0.0)
                    s['he'][g] = new
                    s['l'][g] = jnp.where(lane8 == k, lc, s['l'][g])
                for g in range(tiles):
                    new = s['yw'][g] - cy[g] * un
                    s['yw'][g] = jnp.where(isk, un, new) if g == gk else new
                s['u'][gk] = jnp.where(isk, u, s['u'][gk])
                s['tau'] = jnp.where(lane8 == k, -ukk * rinv, s['tau'])
    out = []
    up = c64 >= r64
    for s in st:
        he = jnp.concatenate(s['he'], 0)
        yw = jnp.concatenate(s['yw'], 0)
        l = jnp.concatenate(s['l'], 0)[:, :W]
        u = jnp.concatenate(s['u'], 0)[:, :W]
        out.append((jnp.where(c64 <= r64, he[:, W:], 0.0), l + eye, jnp.where(up, u, 0.0), yw[:, W:], s['tau'][0:1, :W]))
    return out


def blk(b):
    return slice(b * W, (b + 1) * W)


def order(c):
    return [2 * l + c for l in BOTH] + [2 * l + 1 - c for l in BOTH]


def turn(x):
    return jnp.concatenate([x[:, W:N], x[:, :W], x[:, N:]], 1)


CHAIN_SCRATCH = [(N, 2 * N), (N, 2 * N), (N, N), (4, W, W), (8, N), (8, W)]
CHAIN_SHAPES = [(N, N), (N, N), (2 * W, N), (2 * W, N), (N, W), (NP, W), TILE]


def chain_init(col, g, x1, st):
    hs, ys, ls, _, norm, _ = st
    ri, ci = rows_of((N, N)), lanes_of((N, N))
    eye = (ri == ci).astype(F32)
    for c in BOTH:
        @pl.when(col == c)
        def _():
            for i, b in enumerate(order(c)):
                ls[blk(b), :] = x1[blk(i), :]
                for i2, b2 in enumerate(order(c)):
                    hs[blk(b), blk(b2)] = g[blk(i), blk(i2)]
    hs[:, N:] = eye
    ys[:, :N] = ls[...].T
    ys[:, N:] = eye
    dg = jnp.where(ri == ci, hs[:, :N], 0.0)
    norm[...] = jnp.broadcast_to(jnp.sqrt(jnp.sum(dg, 0, keepdims=True)), (8, N))


def chain_cols(st):
    hs, ys, _, fac, _, tv = st
    e, l, u, w, tau = diag_factor([(hs[0:W, 0:W], ys[0:W, 0:W])])[0]
    for i, x in enumerate((e, l, u, w)):
        fac[i] = x
    tv[...] = jnp.broadcast_to(tau, (8, W))


def chain_update(p, st, tfac, tau):
    hs, ys, ls, fac, _, tv = st
    r64 = rows_of((W, W))
    c64 = lanes_of((W, W))
    rw = rows_of((W, 2 * N))
    cw = lanes_of((W, 2 * N))
    rl = rows_of((N - W, W))
    live = N - p * W
    e, l, u, w = fac[0], fac[1], fac[2], fac[3]
    t = -hdot(hdot(u, e, NT), hdot(u, w), NT)
    d = pl.ds(pl.multiple_of(p * W, W), W)
    tfac[d, :] = jnp.where(c64 > r64, t, jnp.where(c64 == r64, jnp.broadcast_to(tv[0:1, :], (W, W)), 0.0))
    tau[pl.ds(p, 1), :] = tv[0:1, :]
    rall = hdot(e, hs[0:W, :])
    rall = jnp.where((cw >= N) | ((cw >= rw) & (cw < live)), rall, 0.0)
    nrow = hdot(w, ys[0:W, :] - jnp.where(cw < N, rall, 0.0))
    hnew = hs[W:, :] - hdot(rall[:, W:N], rall, TN)
    yc = ys[W:, 0:W]
    ynew = ys[W:, :] - hdot(yc, nrow)
    lnew = jnp.where(rl < live - W, hdot(yc, hdot(w, l)), 0.0)
    rest = ls[W:, W:]
    first = ls[0:W, W:]
    ls[0:N - W, N - W:] = lnew
    ls[N - W:, N - W:] = l
    ls[0:N - W, 0:N - W] = rest
    ls[N - W:, 0:N - W] = first
    hs[0:N - W, :] = turn(hnew)
    hs[N - W:, :] = turn(rall)
    ys[0:N - W, :] = turn(ynew)
    ys[N - W:, :] = turn(nrow)


def chain_final(col, st, outs):
    hs, ys, ls, _, norm, _ = st
    rinvt, minv, upt, ptt, _, _, bad = outs
    ri = rows_of((N, N))
    ci = lanes_of((N, N))
    rt, mi = hs[:, N:], ys[:, N:]
    g = norm[0:1, :]
    c1 = jnp.max(jnp.sum(jnp.abs(rt) * g, 1, keepdims=True), keepdims=True)
    c2 = jnp.max(hdot(g, jnp.abs(mi)), keepdims=True)
    good = (c1 <= AMPLIFY) & (c2 <= AMPLIFY) & (jnp.min(g, keepdims=True) >= 1 / HUGE) & (jnp.max(g, keepdims=True) <= HUGE)
    bad[...] = jnp.broadcast_to(jnp.where(good, 0.0, 1.0), TILE)
    pt = jnp.where(ri > ci, ls[...], hs[:, :N]).T
    ut = lax.dot_general(ls[...], mi, (((0,), (1,)), ((), ())), precision=HI, preferred_element_type=F32)
    hs[:, :N] = pt
    ys[:, :N] = ut
    for c in BOTH:
        @pl.when(col == c)
        def _():
            for i, b in enumerate(order(c)):
                rinvt[:, blk(i)] = hs[:, N + b * W:N + (b + 1) * W]
                minv[blk(i), :] = ys[blk(b), N:]
            for i in BOTH:
                b = order(c)[i]
                ptt[blk(i), :] = hs[blk(b), :N]
                for i2, b2 in enumerate(order(c)):
                    upt[blk(i), blk(i2)] = ys[blk(b), blk(b2)]


def split3(x):
    h = x.astype(BF)
    r = x - h.astype(F32)
    m = r.astype(BF)
    return h, m, (r - m.astype(F32)).astype(BF)


def dot6(a, b, dn):
    d = lambda i, j: lax.dot_general(a[i], b[j], dn, preferred_element_type=F32)
    return (((d(2, 0) + d(0, 2)) + d(1, 1)) + (d(1, 0) + d(0, 1))) + d(0, 0)


CHUNK = 1024
SPAN = 1024
SLOTS = 3
AHEAD = SLOTS - 1


def exchange_kernel(ca, cb, peer_a, peer_b, c1a, c1b, pam, pao, pbm, g_out, x1b, *refs):
    outs, refs = refs[:len(CHAIN_SHAPES)], refs[len(CHAIN_SHAPES):]
    st, refs = refs[:len(CHAIN_SCRATCH)], refs[len(CHAIN_SCRATCH):]
    (x1a, peer, own, xs, cbuf, acc, gacc, r1buf, r2buf, gloc, gbuf1, gsum, gbuf2,
     c_sem, own_sem, out_sem, y_send, y_recv, top_send, top_recv, swap_send, swap_recv,
     g_send, g_recv, p_send, p_recv, x_send, x_recv) = refs
    cts, x1 = (ca, cb), (x1a, x1b)
    row = lax.axis_index("row")
    col = lax.axis_index("col")
    core = lax.rem(row, 2)
    mate = row + 1 - 2 * core
    across = lax.rem(row + 2, 4)
    diag = lax.rem(row + 3 - 2 * core, 4)
    cols, rows = ca.shape
    half = cols // 2
    nown = peer.shape[1]
    nchunk = cols // CHUNK
    spans = rows // SPAN
    trips = nchunk * spans

    def remote(src, dst, send, recv, **where):
        return pltpu.make_async_remote_copy(src_ref=src, dst_ref=dst, send_sem=send, recv_sem=recv,
                                            device_id=where, device_id_type=pl.DeviceIdType.MESH)

    to_mate = functools.partial(remote, row=mate)
    to_across = functools.partial(remote, row=across)

    def c_copy(m, t):
        slot = lax.rem(m * trips + t, SLOTS)
        h, j = lax.div(t, nchunk), lax.rem(t, nchunk)
        return pltpu.make_async_copy(
            cts[m].at[pl.ds(pl.multiple_of(j * CHUNK, CHUNK), CHUNK), pl.ds(pl.multiple_of(h * SPAN, SPAN), SPAN)],
            cbuf.at[slot], c_sem.at[slot])

    first = pl.ds(0, nown)
    second = pl.ds(nown, nown)
    lanes = pl.ds(0, N)

    def y_copy(m, h):
        s = pl.ds(pl.multiple_of(h * SPAN, SPAN), SPAN)
        i = m * spans + h
        return remote(cts[m].at[first, s], peer.at[m, :, s], y_send.at[i], y_recv.at[i], col=1 - col)

    own_copies = [pltpu.make_async_copy(cts[m].at[first, :], own.at[m], own_sem.at[m]) for m in BOTH]
    for o in own_copies:
        o.start()
    for t in range(AHEAD):
        c_copy(0, t).start()

    barrier = pltpu.get_barrier_semaphore()
    for where in (dict(row=mate), dict(row=across), dict(row=diag), dict(col=1 - col)):
        pl.semaphore_signal(barrier, device_id=where, device_id_type=pl.DeviceIdType.MESH)
    pl.semaphore_wait(barrier, 4)

    for m in BOTH:
        for h in range(spans):
            y_copy(m, h).start()

    tops = (c1a, c1b)
    lows = [pl.ds(0, half), pl.ds(half, half)]
    x_local = [pltpu.make_async_copy(cts[m].at[first, lanes], x1[m].at[first, :], own_sem.at[2 + m]) for m in BOTH]
    x_own = [[remote(cts[m].at[first, lanes], x1[m].at[first, :], top_send.at[m, k], top_recv.at[m], row=k + 1)
              for k in range(3)] for m in BOTH]
    x_peer = [[remote(peer.at[m, :, lanes], x1[m].at[second, :], top_send.at[2 + m, k], top_recv.at[2 + m], row=k + 1)
               for k in range(3)] for m in BOTH]
    top_far = [[remote(cts[m].at[:, lanes], tops[m], top_send.at[4 + m, 0], top_recv.at[4 + m], row=1)]
               + [remote(cts[m].at[lows[k], lanes], tops[m].at[lows[k], :], top_send.at[4 + m, 1 + k], top_recv.at[4 + m], row=2 + k)
                  for k in BOTH] for m in BOTH]

    @pl.when(row == 0)
    def _():
        for m in BOTH:
            x_local[m].start()
        for c in x_own[0] + x_own[1] + top_far[0] + top_far[1]:
            c.start()

    mine = pl.ds(pl.multiple_of(core * half, half), half)
    others = pl.ds(pl.multiple_of((1 - core) * half, half), half)
    p1 = [to_mate(acc.at[m, others, :], r1buf.at[m], p_send.at[m], p_recv.at[m]) for m in BOTH]
    g1 = [to_mate(gloc.at[m], gbuf1.at[m], g_send.at[m], g_recv.at[m]) for m in BOTH]
    g2 = [to_across(gsum.at[m], gbuf2.at[m], g_send.at[2 + m], g_recv.at[2 + m]) for m in BOTH]
    p2 = to_across(r1buf.at[0], r2buf, x_send.at[0], x_recv.at[0])
    p3 = to_mate(r1buf.at[0], pao, x_send.at[1], x_recv.at[1])
    swap = [to_mate(tops[m].at[mine, :], tops[m].at[mine, :], swap_send.at[m], swap_recv.at[m]) for m in BOTH]
    peer_out = [pltpu.make_async_copy(peer.at[m], (peer_a, peer_b)[m], out_sem.at[m]) for m in BOTH]
    pam_out = pltpu.make_async_copy(r1buf.at[0], pam, out_sem.at[2])
    pbm_out = pltpu.make_async_copy(r1buf.at[1], pbm, out_sem.at[3])

    def add_half(m):
        p1[m].wait()
        r1buf[m] = r1buf[m] + acc[m, mine, :]

    def start_g(m):
        gloc[m, 0:nown, :] = acc[m, 0:nown, :]
        gloc[m, nown:, :] = gacc[m]
        g1[m].start()

    def finish_g1(m):
        g1[m].wait()
        gsum[m] = gloc[m] + gbuf1[m]
        g2[m].start()

    def send_x(m):
        @pl.when(row == 0)
        def _():
            x1[m][nown:, :] = peer[m, :, 0:N]
            for c in x_peer[m]:
                c.start()

    def wait_x(m):
        @pl.when(row == 0)
        def _():
            x_local[m].wait()

        @pl.when(row > 0)
        def _():
            x_own[m][0].wait_recv()
            x_peer[m][0].wait_recv()

    def sums_a():
        finish_g1(0)
        add_half(0)
        p2.start()

    def begin_chain():
        wait_x(0)
        g2[0].wait()
        gsum[0] = gsum[0] + gbuf2[0]
        chain_init(col, gsum.at[0], x1a, st)

    def top_rows():
        @pl.when(row == 1)
        def _():
            for m in BOTH:
                top_far[m][0].wait_recv()

        @pl.when(row >= 2)
        def _():
            for m in BOTH:
                top_far[m][1].wait_recv()
                swap[m].start()

    def finish_chain():
        chain_final(col, st, outs)
        top_rows()

    def last_sums_a():
        p2.wait()
        r1buf[0] = r1buf[0] + r2buf[...]
        p3.start()
        pam_out.start()

    last = trips - nchunk
    begin = last - NP
    hooks = [[(0, lambda: send_x(0))],
             [(0, lambda: send_x(1)), (begin - 1, begin_chain), (last - 2, last_sums_a), (last - 1, finish_chain),
              (last, lambda: start_g(1))]]

    def products(m):
        def span(h, _):
            y_copy(m, h).wait_recv()
            s0 = pl.multiple_of(h * SPAN, SPAN)

            def build(q, _):
                d = pl.ds(pl.multiple_of(q * 512, 512), 512)
                s = pl.ds(pl.multiple_of(s0 + q * 512, 512), 512)
                for i, part in enumerate(split3(own[m, :, s])):
                    xs[i, 0:nown, d] = part
                for i, part in enumerate(split3(peer[m, :, s])):
                    xs[i, nown:, d] = part
                return 0

            lax.fori_loop(0, SPAN // 512, build, 0)
            x = (xs[0], xs[1], xs[2])
            r = dot6([xs[i, nown:, :] for i in range(3)], x, NT)
            gacc[m] = jnp.where(h == 0, r, gacc[m] + r)

            def trip(j, _):
                t = h * nchunk + j
                slot = lax.rem(m * trips + t, SLOTS)
                c_copy(m, t).wait()

                @pl.when(t + AHEAD < trips)
                def _():
                    c_copy(m, t + AHEAD).start()

                if m == 0:
                    @pl.when(t + AHEAD >= trips)
                    def _():
                        c_copy(1, t + AHEAD - trips).start()

                def core_trip():
                    r = dot6(split3(cbuf[slot]), (xs[0], xs[1], xs[2]), NT)
                    d = pl.ds(pl.multiple_of(j * CHUNK, CHUNK), CHUNK)
                    acc[m, d, :] = jnp.where(h == 0, r, acc[m, d, :] + r)

                if m == 0:
                    core_trip()
                else:
                    live = (t >= begin) & (t < last)

                    @pl.when(live)
                    def _():
                        chain_cols(st)
                        core_trip()
                        chain_update(t - begin, st, outs[4], outs[5])

                    pl.when(~live)(core_trip)
                for at, hook in hooks[m]:
                    pl.when(t == at)(hook)
                return 0

            lax.fori_loop(0, nchunk, trip, 0)
            return 0

        own_copies[m].wait()
        lax.fori_loop(0, spans, span, 0)

    products(0)
    start_g(0)
    p1[0].start()
    peer_out[0].start()
    sums_a()
    products(1)
    p1[1].start()
    finish_g1(1)
    peer_out[1].start()
    wait_x(1)
    add_half(1)
    pbm_out.start()
    g2[1].wait()
    g_out[...] = gsum[1] + gbuf2[1]

    @pl.when(row == 0)
    def _():
        for c in x_own[0] + x_own[1] + x_peer[0] + x_peer[1] + top_far[0] + top_far[1]:
            c.wait_send()

    @pl.when(row >= 2)
    def _():
        for m in BOTH:
            swap[m].wait()

    for c in peer_out + [p3, pam_out, pbm_out]:
        c.wait()
    for m in BOTH:
        for h in range(spans):
            y_copy(m, h).wait_send()


def exchange(ca, cb, own):
    cols, rows = ca.shape
    half = cols // 2
    hbm = pl.BlockSpec(memory_space=pl.ANY)
    vm = pl.BlockSpec(memory_space=pltpu.VMEM)
    dma = pltpu.SemaphoreType.DMA
    pair = (2, N, N)
    ny = 2 * rows // SPAN
    shapes = [(own, rows)] * 2 + [(cols, N)] * 2 + [(half, N)] * 3 + [(N, N), (N, N)] + CHAIN_SHAPES
    scratch = CHAIN_SCRATCH + [(N, N), (2, own, rows), (2, own, rows)]
    after = [(SLOTS, CHUNK, SPAN), (2, cols, N), (2, own, N), (2, half, N), (half, N)] + [pair] * 4
    return pl.pallas_call(
        exchange_kernel,
        in_specs=[hbm, hbm],
        out_specs=[hbm] * 7 + [vm] * (2 + len(CHAIN_SHAPES)),
        out_shape=[jax.ShapeDtypeStruct(s, F32) for s in shapes],
        scratch_shapes=[pltpu.VMEM(s, F32) for s in scratch] + [pltpu.VMEM((3, 2 * own, SPAN), BF)]
        + [pltpu.VMEM(s, F32) for s in after]
        + [dma(n) for n in ((SLOTS,), (4,), (4,), (ny,), (ny,), (6, 3), (6,), (2,), (2,), (4,), (4,), (2,), (2,), (2,), (2,))],
        cost_estimate=pl.CostEstimate(flops=24 * cols * rows * N, bytes_accessed=8 * cols * rows, transcendentals=0),
        compiler_params=pltpu.CompilerParams(vmem_limit_bytes=60 * 2**20, collective_id=0, has_side_effects=True))(ca, cb)


def apply_update(ids, ct, peer, psum, poth, c1, small, before, nxt=None):
    cols, rows = ct.shape
    nb = 512
    mb = 512
    own = peer.shape[0]
    half = cols // 2
    steps = rows // nb
    rinvt, minv, upt, ptt, _, _, bad = small
    no = len(CHAIN_SHAPES)

    def body(ids_ref, c_ref, x_ref, p_ref, q_ref, c1_ref, r_ref, m_ref, up_ref, pt_ref, bad_ref, before_ref, *refs):
        if nxt is None:
            o_ref, f_ref, z_ref, rc_ref = refs
        else:
            ins, (o_ref, f_ref), outs, (z_ref, rc_ref), st = refs[:2], refs[2:4], refs[4:4 + no], refs[4 + no:6 + no], refs[6 + no:]
        i = pl.program_id(0)
        top = ids_ref[0] == 0

        @pl.when(i == 0)
        def _():
            zero = jnp.zeros((1, 1), F32)
            for src, which in ((p_ref, 0), (q_ref, 1)):
                base = pl.multiple_of((ids_ref[1] ^ which) * half, half)
                for j in range(half // mb):
                    s = slice(j * mb, (j + 1) * mb)
                    d = pl.ds(base + j * mb, mb)
                    rc = hdot(src[s, :], r_ref[...], NT)
                    z = hdot(jnp.where(top, c_ref[d, 0:N], c1_ref[d, :]) - rc, m_ref[...], NT)
                    rc_ref[d, :] = rc
                    z_ref[d, :] = z
                    zero = zero + jnp.sum(jnp.sum(z * 0.0, 0, keepdims=True), 1, keepdims=True)
            f_ref[...] = jnp.where(zero == 0.0, 0.0, 1.0) + bad_ref[...] + before_ref[...]
            if nxt is not None:
                chain_init(ids_ref[2], *ins, st)

        def products():
            x = jnp.concatenate([c_ref[0:own, :], x_ref[...]], 0)
            o_ref[0:own, :] = hdot(up_ref[...], x)
            o_ref[own:mb, :] = c_ref[own:mb, :] - hdot(z_ref[own:mb, :], x)
            for j in range(1, cols // mb):
                s = slice(j * mb, (j + 1) * mb)
                o_ref[s, :] = c_ref[s, :] - hdot(z_ref[s, :], x)

        if nxt is None:
            products()
        else:
            @pl.when(lax.rem(i, 2) == 0)
            def _():
                chain_cols(st)
                products()

            @pl.when(lax.rem(i, 2) == 1)
            def _():
                products()
                chain_update(lax.div(i, 2), st, outs[4], outs[5])

            @pl.when(i == steps - 1)
            def _():
                chain_final(ids_ref[2], st, outs)

        @pl.when((i == 0) & top)
        def _():
            o_ref[0:own, 0:N] = pt_ref[...]
            o_ref[own:, 0:N] = rc_ref[own:, :]

    blk2 = pl.BlockSpec((cols, nb), lambda i, r: (0, i))
    fixed = lambda shape: pl.BlockSpec(shape, lambda i, r: (0, 0))
    consts = [psum, poth, c1, rinvt, minv, upt, ptt, bad, before] + list(nxt or [])
    more = CHAIN_SHAPES if nxt is not None else []
    scratch = [(cols, N), (cols, N)] + (CHAIN_SCRATCH if nxt is not None else [])
    return pl.pallas_call(
        body,
        grid_spec=pltpu.PrefetchScalarGridSpec(
            num_scalar_prefetch=1, grid=(steps,),
            in_specs=[blk2, pl.BlockSpec((own, nb), lambda i, r: (0, i))] + [fixed(a.shape) for a in consts],
            out_specs=[blk2, fixed((8, 128))] + [fixed(s) for s in more],
            scratch_shapes=[pltpu.VMEM(s, F32) for s in scratch]),
        out_shape=[jax.ShapeDtypeStruct(s, F32) for s in [(cols, rows), (8, 128)] + more],
        cost_estimate=pl.CostEstimate(flops=2 * 6 * cols * rows * N, bytes_accessed=8 * cols * rows, transcendentals=0),
        compiler_params=pltpu.CompilerParams(vmem_limit_bytes=60 * 2**20))(ids, ct, peer, *consts)


R1 = [(0, 1), (1, 0), (2, 3), (3, 2)]
R2 = [(0, 2), (2, 0), (1, 3), (3, 1)]
CY = [(0, 1), (1, 0)]


def row_major(x):
    def body(i_ref, o_ref):
        o_ref[...] = i_ref[...]

    return pl.pallas_call(body, out_shape=jax.ShapeDtypeStruct(x.shape, F32))(x)


def row_sum(x):
    x = x + lax.ppermute(x, "row", R1)
    return x + lax.ppermute(x, "row", R2)


def factor_columns(stored):
    local_rows, local_blocks, width = stored.shape
    row_rank = lax.axis_index("row")
    col_rank = lax.axis_index("col")
    row_ids = row_rank * local_rows + jnp.arange(local_rows)
    col_ids = jnp.arange(width)
    edot = functools.partial(jnp.einsum, precision=HI, preferred_element_type=F32)

    def panel_step(panel_idx, state):
        stored, taus, tfs = state
        row_start = panel_idx * width
        local_idx = panel_idx // 2
        is_owner = col_rank == panel_idx % 2
        panel_in = lax.dynamic_slice_in_dim(stored, local_idx, 1, axis=1)[:, 0, :]

        def column_step(col_idx, loop_state):
            work, tau_vec = loop_state
            diag_idx = row_start + col_idx
            column = lax.dynamic_slice_in_dim(work, col_idx, 1, axis=1)[:, 0]
            below = jnp.where(row_ids >= diag_idx, column, 0.0)
            at_diag = (row_ids == diag_idx).astype(F32)
            summed = row_sum(edot("ar,rk->ak", jnp.stack([below, at_diag]), work))
            cross, diag_row = summed[0], summed[1]
            pivot = lax.dynamic_slice_in_dim(diag_row, col_idx, 1)[0]
            norm = jnp.sqrt(lax.dynamic_slice_in_dim(cross, col_idx, 1)[0])
            beta = -jnp.where(pivot >= 0, 1.0, -1.0) * norm
            tau = (beta - pivot) / beta
            denom = pivot - beta
            proj = jnp.where(col_ids > col_idx, (cross - beta * diag_row) / denom, 0.0)
            refl = jnp.where(row_ids > diag_idx, column / denom, 0.0) + at_diag
            work = work - tau * refl[:, None] * proj[None, :]
            new_col = jnp.where(row_ids < diag_idx, column, jnp.where(row_ids == diag_idx, beta, refl))
            work = lax.dynamic_update_slice_in_dim(work, new_col[:, None], col_idx, axis=1)
            return work, lax.dynamic_update_slice_in_dim(tau_vec, tau[None], col_idx, axis=0)

        work, tau_vec = lax.fori_loop(0, width, column_step, (panel_in, jnp.zeros((width,), F32)))
        diag_ids = row_start + col_ids[None, :]
        v_block = jnp.where(row_ids[:, None] == diag_ids, 1.0, jnp.where(row_ids[:, None] > diag_ids, work, 0.0))
        gram = row_sum(edot("ri,rj->ij", v_block, v_block))

        def t_step(col_idx, tf):
            g = lax.dynamic_slice_in_dim(gram, col_idx, 1, axis=1)[:, 0]
            g = jnp.where(col_ids < col_idx, g, 0.0)
            tau_k = lax.dynamic_slice_in_dim(tau_vec, col_idx, 1)[0]
            t_col = -tau_k * edot("ij,j->i", tf, g)
            t_col = jnp.where(col_ids == col_idx, tau_k, t_col)
            return lax.dynamic_update_slice_in_dim(tf, t_col[:, None], col_idx, axis=1)

        tf = lax.fori_loop(0, width, t_step, jnp.zeros((width, width), F32))
        v_mine = jnp.where(is_owner, v_block, 0.0)
        t_mine = jnp.where(is_owner, tf, 0.0)
        v_block = v_mine + lax.ppermute(v_mine, "col", CY)
        tf = t_mine + lax.ppermute(t_mine, "col", CY)

        def block_step(b, stored):
            blk = lax.dynamic_slice_in_dim(stored, b, 1, axis=1)[:, 0, :]
            w = edot("ij,ik->jk", tf, row_sum(edot("ri,rk->ik", v_block, blk)))
            upd = blk - edot("ri,ik->rk", v_block, w)
            keep = b * 2 + col_rank > panel_idx
            mine = (b == local_idx) & is_owner
            new = jnp.where(keep, upd, jnp.where(mine, work, blk))
            return lax.dynamic_update_slice_in_dim(stored, new[:, None, :], b, axis=1)

        stored = lax.fori_loop(0, local_blocks, block_step, stored)
        taus = lax.dynamic_update_slice_in_dim(taus, jnp.diagonal(tf), row_start, axis=0)
        return stored, taus, lax.dynamic_update_slice_in_dim(tfs, tf, row_start, axis=0)

    return lax.fori_loop(0, PANELS, panel_step, (stored, jnp.zeros((PANELS * width,), F32), jnp.zeros((PANELS * width, width), F32)))


def solution(mesh):
    def factor_both(a_matrix, b_matrix):
        local_rows, local_blocks, width = a_matrix.shape
        cols = local_blocks * width
        own = 2 * width
        row_rank = lax.axis_index("row")
        col_rank = lax.axis_index("col")
        core = row_rank % 2
        cts = [m.transpose(1, 2, 0).reshape(cols, local_rows) for m in (a_matrix, b_matrix)]

        pa, pb, c1a, c1b, pam, pao, pbm, g, x1, *first = exchange(*cts, own)
        across = lax.ppermute(pbm, "row", R2)
        ids = jnp.stack([row_rank, core, col_rank]).astype(jnp.int32)
        out_a, bad_a, *second = apply_update(ids, cts[0], pa, pam, pao, c1a, first, jnp.zeros(TILE, F32), (g, x1))
        across, bad_a = lax.optimization_barrier((across, bad_a))
        pbm = pbm + across
        pbo = lax.ppermute(pbm, "row", R1)
        tt = jnp.concatenate([s[i] for s in (first, second) for i in (4, 5)], 0)
        tt = jnp.where(col_rank == 0, tt, lax.ppermute(tt, "col", [(0, 1)]))
        out_b, bad = apply_update(ids, cts[1], pb, pbm, pbo, c1b, second, bad_a)
        bad = bad + lax.ppermute(bad, "col", CY)
        carry = [bad]
        for i, out in enumerate((out_a, out_b)):
            at = i * (N + NP)
            carry += [out, tt[at + N:at + N + NP], tt[at:at + N]]

        def redo(state):
            new = [jnp.zeros(TILE, F32)]
            for m in (a_matrix, b_matrix):
                st, taus, tfs = factor_columns(m)
                new += [st.transpose(1, 2, 0).reshape(cols, local_rows), row_major(taus.reshape(NP, W)), row_major(tfs)]
            return tuple(new)

        res = lax.while_loop(lambda s: s[0][0, 0] > 0.5, redo, tuple(carry))
        back = lambda x: x.reshape(local_blocks, width, local_rows).transpose(2, 0, 1)
        stack = lambda t: t.reshape(PANELS, width, width)
        return back(res[1]), res[2].reshape(N), stack(res[3]), back(res[4]), res[5].reshape(N), stack(res[6])

    spec_mat = P(("batch", "row"), "col", None)
    spec_out = (spec_mat, P("batch"), P("batch", None, None))
    return jax.shard_map(factor_both, mesh=mesh, in_specs=(spec_mat, spec_mat), out_specs=spec_out + spec_out, check_vma=False)
```

time: 8330 us -> 241 us (0.03)
  blocking collectives: 3160 us -> 0 us
  matrix products: 1850 us -> 0 us
  loops' own time: 1720 us -> 1.68 us
  local copies, waits for them, and re-layouts: 963 us -> 5.75 us
  other arithmetic: 501 us -> 4.16 us
  Pallas kernels: 0 us -> 211 us
    psum x520 -> x0, blocking collectives: 3160 us -> none  [the longest x512 3080 us: column_step(): summed = lax.psum(part_sums, 'row')]
    another operation x16 -> x1, loops' own time: 1720 us -> 1.68 us  [factor_both(): res = lax.while_loop(lambda s: s[0][0, 0] > 0.5, redo, tuple(carry))]
    dot_general x1560 -> x0, matrix products: 1610 us -> none  [the longest x512 469 us: column_step(): jnp.dot(below_diag, panel_work, precision=PRECISE, preferred_element_type...]
    dynamic_slice x1536 -> x0, local copies, waits for them, and re-layouts: 642 us -> none  [the longest x512 323 us: column_step(): pivot_val = lax.dynamic_slice_in_dim(diag_row, col_idx, 1)[0]]
    dynamic_update_slice x1536 -> x0, local copies, waits for them, and re-layouts: 273 us -> none  [the longest x512 201 us: column_step(): lax.dynamic_update_slice_in_dim(panel_work, new_col[:, None], col_idx, ax...]
    unnamed x8 -> x0, matrix products: 243 us -> none
    pallas_call x0 -> x3, Pallas kernels: none -> 211 us  [the longest x1 120 us: exchange(): pl.pallas_call(exchange_kernel, in_specs=[hbm, hbm], out_specs=[hbm] * 7...]
    select_n x1037 -> x1, other arithmetic: 179 us -> 0.97 us  [factor_both(): tt = jnp.where(col_rank == 0, tt, lax.ppermute(tt, 'col', [(0, 1)]))]
where the time goes in v1:
time: 241 us; the launch traced here: 237 us
  Pallas kernels  211 us (88%)
  waiting for transfers between devices  7.02 us (3%)
  starting transfers between devices  6.46 us (3%)
  local copies, waits for them, and re-layouts  5.75 us (2%)
  other arithmetic  4.16 us (2%)
    pallas_call x1, Pallas kernels, exchange(): pl.pallas_call(exchange_kernel, in_specs=[hbm, hbm], out_specs=[hbm] * 7...  120 us
    pallas_call x2, Pallas kernels, apply_update(): pl.pallas_call(body, grid_spec=pltpu.PrefetchScalarGridSpec(num_scalar_pr...  90.4 us
    ppermute x1, waiting for transfers between devices, factor_both(): tt = jnp.where(col_rank == 0, tt, lax.ppermute(tt, 'col', [(0, 1)]))  6.03 us
  transfers between devices with their start and end apart: 4, of which 2 were waited for; matrix products, arithmetic and copies ran while one was open for 2% of the time, Pallas kernels for 21%

profile of v1, /device:TPU:0, one launch (start us, length us, event | category | flops | bytes accessed | tf_op | source)
XLA Modules:
  0.0 236.9 jit_solution(10484721402527554473)
XLA Ops:
  0.6 120.4 %shard_map.73 = (f32[128,4096]{1,0:T(8,128)}, f32[128,4096]{1,0:T(8,128)}, f32[2048,256]{1,0:T(8,128)}, f32[2048,256]{1,0:T(8,128)}, f32[1024,256]{1,0:T(8,128)}...) custom-call(f32[2048,4096]{1,0:T(8,128)} %bitcast.269, ...), custom_call_target="tpu_custom_call" | custom-call | flops 51539607552 | bytes 67108864 | tf_op jit(solution)/shard_map/pallas_call | solution.py:492
  121.1 1.5 collective-permute-start.16
  122.6 0.6 pad_add_fusion.ids_ref
  123.2 0.6 broadcast_19_before_ref.2.before_ref
  123.8 0.0 copy-start.2
  123.8 0.0 copy-start.4
  123.8 0.0 copy-start.5
  123.8 50.0 %shard_map.74 = (f32[2048,4096]{1,0:T(8,128)}, f32[8,128]{1,0:T(8,128)}, f32[256,256]{1,0:T(8,128)}, f32[256,256]{1,0:T(8,128)}, f32[128,256]{1,0:T(8,128)}, /*i...) custom-call(s32[3]{0:T(128)} %pad_add_fusion.ids_ref, f32[2048,4096]{1,0:T(8,128)} %bitcast.270, ...), custom_call_target="tpu_custom_call" | custom-call | flops 25769803776 | bytes 67108864 | tf_op jit(solution)/shard_map/pallas_call | solution.py:574
  173.7 0.0 collective-permute-done.16
  173.8 0.0 copy-done.2
  173.8 0.1 add.522.p_ref
  173.9 0.0 copy-start.3
  173.9 0.0 collective-permute-start.17
  174.0 0.0 copy-done.4
  174.0 0.0 copy-done.5
  174.0 1.2 pad_maximum_fusion
  175.1 2.4 %collective-permute-start.19 = (f32[520,64]{1,0:T(8,128)S(1)}, f32[520,64]{1,0:T(8,128)S(1)}, u32[]{:S(2)}, u32[]{:S(2)}) collective-permute-start(f32[520,64]{1,0:T(8,128)S(1)} %pad_maximum_fusion), channel_id=1, source_target_pairs={{0,4},{1,5},{2,6},{3,7}} | collective-permute-start | bytes 399368 | tf_op jit(solution)/shard_map/ppermute | solution.py:691
  177.6 6.0 %collective-permute-done.19 = f32[520,64]{1,0:T(8,128)S(1)} collective-permute-done((f32[520,64]{1,0:T(8,128)S(1)}, f32[520,64]{1,0:T(8,128)S(1)}, u32[]{:S(2)}, u32[]{:S(2)}) %collective-permute-start.19) | collective-permute-done | bytes 133152 | tf_op jit(solution)/shard_map/ppermute | solution.py:691
  183.6 1.0 broadcast_select_fusion.2
  184.6 0.7 fusion.82
  185.3 0.0 collective-permute-done.17.q_ref
  185.3 0.0 copy-done.3
  185.3 40.5 %shard_map.75 = (f32[2048,4096]{1,0:T(8,128)}, f32[8,128]{1,0:T(8,128)}) custom-call(s32[3]{0:T(128)} %pad_add_fusion.ids_ref, f32[2048,4096]{1,0:T(8,128)} %bitcast.268, f32[128,4096]{1,0:T(8,128)} %get-tuple-element.1420.x_ref, f32[1024,256]{1,0:T(8,128)} %copy-done.3, f32[1024,256]{1,0:T(8,128)} %collective-permute-done.17.q_ref, ...), custom_call_target="tpu_custom_call" | custom-call | flops 25769803776 | bytes 67108864 | tf_op jit(solution)/shard_map/pallas_call | solution.py:574
  225.7 2.5 %collective-permute-start.18 = (f32[8,128]{1,0:T(8,128)}, f32[8,128]{1,0:T(8,128)S(1)}, u32[]{:S(2)}, u32[]{:S(2)}) collective-permute-start(f32[8,128]{1,0:T(8,128)} %get-tuple-element.1442), channel_id=1, source_target_pairs={{0,4},{4,0},{1,5},{5,1},{2,6},{6,2},{3,7},{7,3}} | collective-permute-start | bytes 12296 | tf_op jit(solution)/shard_map/ppermute | solution.py:693
  228.3 0.6 fusion.83
  228.9 1.0 collective-permute-done.18
  229.8 1.3 add.523
  231.1 2.9 %while.319 = (f32[8,128]{1,0:T(8,128)}, f32[2048,4096]{1,0:T(8,128)}, f32[4,64]{1,0:T(4,128)}, f32[256,64]{1,0:T(8,128)}, f32[2048,4096]{1,0:T(8,128)}, /*index=...) while((f32[8,128]{1,0:T(8,128)}, ...), condition=%wide.region_17.18_spmd, body=%wide.region_0.17_spmd.sunk | while | flops 1237608960 | bytes 197574640 | solution.py:706
  231.1 1.2 slice.78
  234.0 1.3 reshape.265
  235.3 1.3 reshape.268
Async XLA Ops:
  121.1 52.7 %collective-permute-start.16 = (f32[1024,256]{1,0:T(8,128)}, f32[1024,256]{1,0:T(8,128)S(1)}, u32[]{:S(2)}, u32[]{:S(2)}) collective-permute-start(f32[1024,256]{1,0:T(8,128)} %get-tuple-element.1421), channel_id=1, source_target_pairs={{0,2},{2,0},{1,3},{3,1},{4,6},{6,4},{5,7},{7,5}} | collective-permute-start | bytes 3145736 | tf_op jit(solution)/shard_map/ppermute | solution.py:684
  123.8 50.0 %copy-start.2 = (f32[1024,256]{1,0:T(8,128)S(1)}, f32[1024,256]{1,0:T(8,128)}, u32[]{:S(2)}) copy-start(f32[1024,256]{1,0:T(8,128)} %get-tuple-element.1421) | copy-start | bytes 3145732
  123.8 50.2 %copy-start.4 = (f32[256,64]{1,0:T(8,128)S(1)}, f32[256,64]{1,0:T(8,128)}, u32[]{:S(2)}) copy-start(f32[256,64]{1,0:T(8,128)} %get-tuple-element.1444) | copy-start | bytes 196612
  123.8 50.2 %copy-start.5 = (f32[4,64]{1,0:T(4,128)S(1)}, f32[4,64]{1,0:T(4,128)}, u32[]{:S(2)}) copy-start(f32[4,64]{1,0:T(4,128)} %get-tuple-element.1445) | copy-start | bytes 3076
  173.9 11.4 %copy-start.3 = (f32[1024,256]{1,0:T(8,128)}, f32[1024,256]{1,0:T(8,128)S(1)}, u32[]{:S(2)}) copy-start(f32[1024,256]{1,0:T(8,128)S(1)} %add.522.p_ref) | copy-start | bytes 3145732
  173.9 11.4 %collective-permute-start.17 = (f32[1024,256]{1,0:T(8,128)S(1)}, f32[1024,256]{1,0:T(8,128)}, u32[]{:S(2)}, u32[]{:S(2)}) collective-permute-start(f32[1024,256]{1,0:T(8,128)S(1)} %add.522.p_ref), channel_id=1, source_target_pairs={{0,1},{1,0},{2,3},{3,2},{4,5},{5,4},{6,7},{7,6}} | collective-permute-start | bytes 3145736 | tf_op jit(solution)/shard_map/ppermute | solution.py:689
  175.1 8.5 %collective-permute-start.19 = (f32[520,64]{1,0:T(8,128)S(1)}, f32[520,64]{1,0:T(8,128)S(1)}, u32[]{:S(2)}, u32[]{:S(2)}) collective-permute-start(f32[520,64]{1,0:T(8,128)S(1)} %pad_maximum_fusion), channel_id=1, source_target_pairs={{0,4},{1,5},{2,6},{3,7}} | collective-permute-start | bytes 399368 | tf_op jit(solution)/shard_map/ppermute | solution.py:691
  225.7 4.1 %collective-permute-start.18 = (f32[8,128]{1,0:T(8,128)}, f32[8,128]{1,0:T(8,128)S(1)}, u32[]{:S(2)}, u32[]{:S(2)}) collective-permute-start(f32[8,128]{1,0:T(8,128)} %get-tuple-element.1442), channel_id=1, source_target_pairs={{0,4},{4,0},{1,5},{5,1},{2,6},{6,2},{3,7},{7,3}} | collective-permute-start | bytes 12296 | tf_op jit(solution)/shard_map/ppermute | solution.py:693

commit v2 on v1

--- a/solution.py
+++ b/solution.py
@@ -159,27 +159,39 @@
     rl = rows_of((N - W, W))
     live = N - p * W
     e, l, u, w = fac[0], fac[1], fac[2], fac[3]
-    t = -hdot(hdot(u, e, NT), hdot(u, w), NT)
     d = pl.ds(pl.multiple_of(p * W, W), W)
+    rall = hdot(e, hs[0:W, :])
+    rall = jnp.where((cw >= N) | ((cw >= rw) & (cw < live)), rall, 0.0)
+    ue, uw, wl = hdot(u, e, NT), hdot(u, w), hdot(w, l)
+    yield
+    yc = ys[W:, 0:W]
+    nrow = hdot(w, ys[0:W, :] - jnp.where(cw < N, rall, 0.0))
+    hnew = hs[W:, :] - hdot(rall[:, W:N], rall, TN)
+    hs[0:N - W, :] = turn(hnew)
+    hs[N - W:, :] = turn(rall)
+    t = -hdot(ue, uw, NT)
     tfac[d, :] = jnp.where(c64 > r64, t, jnp.where(c64 == r64, jnp.broadcast_to(tv[0:1, :], (W, W)), 0.0))
     tau[pl.ds(p, 1), :] = tv[0:1, :]
-    rall = hdot(e, hs[0:W, :])
-    rall = jnp.where((cw >= N) | ((cw >= rw) & (cw < live)), rall, 0.0)
-    nrow = hdot(w, ys[0:W, :] - jnp.where(cw < N, rall, 0.0))
-    hnew = hs[W:, :] - hdot(rall[:, W:N], rall, TN)
-    yc = ys[W:, 0:W]
-    ynew = ys[W:, :] - hdot(yc, nrow)
-    lnew = jnp.where(rl < live - W, hdot(yc, hdot(w, l)), 0.0)
+    lnew = jnp.where(rl < live - W, hdot(yc, wl), 0.0)
     rest = ls[W:, W:]
     first = ls[0:W, W:]
     ls[0:N - W, N - W:] = lnew
     ls[N - W:, N - W:] = l
     ls[0:N - W, 0:N - W] = rest
     ls[N - W:, 0:N - W] = first
-    hs[0:N - W, :] = turn(hnew)
-    hs[N - W:, :] = turn(rall)
+    yield
+    ynew = ys[W:, :] - hdot(yc, nrow)
     ys[0:N - W, :] = turn(ynew)
     ys[N - W:, :] = turn(nrow)
+
+
+def weave(stages, pieces):
+    stages = iter(stages)
+    for piece in pieces:
+        next(stages, None)
+        piece()
+    for _ in stages:
+        pass
 
 
 def chain_final(col, st, outs):
@@ -223,6 +235,7 @@
 
 
 CHUNK = 1024
+PIECE = 512
 SPAN = 1024
 SLOTS = 3
 AHEAD = SLOTS - 1
@@ -231,7 +244,7 @@
 def exchange_kernel(ca, cb, peer_a, peer_b, c1a, c1b, pam, pao, pbm, g_out, x1b, *refs):
     outs, refs = refs[:len(CHAIN_SHAPES)], refs[len(CHAIN_SHAPES):]
     st, refs = refs[:len(CHAIN_SCRATCH)], refs[len(CHAIN_SCRATCH):]
-    (x1a, peer, own, xs, cbuf, acc, gacc, r1buf, r2buf, gloc, gbuf1, gsum, gbuf2,
+    (x1a, peer, own, xs, cbuf, acc, gacc, r1buf, r2buf, gbuf1, gsum, gbuf2,
      c_sem, own_sem, out_sem, y_send, y_recv, top_send, top_recv, swap_send, swap_recv,
      g_send, g_recv, p_send, p_recv, x_send, x_recv) = refs
     cts, x1 = (ca, cb), (x1a, x1b)
@@ -307,7 +320,7 @@
     mine = pl.ds(pl.multiple_of(core * half, half), half)
     others = pl.ds(pl.multiple_of((1 - core) * half, half), half)
     p1 = [to_mate(acc.at[m, others, :], r1buf.at[m], p_send.at[m], p_recv.at[m]) for m in BOTH]
-    g1 = [to_mate(gloc.at[m], gbuf1.at[m], g_send.at[m], g_recv.at[m]) for m in BOTH]
+    g1 = [to_mate(gacc.at[m], gbuf1.at[m], g_send.at[m], g_recv.at[m]) for m in BOTH]
     g2 = [to_across(gsum.at[m], gbuf2.at[m], g_send.at[2 + m], g_recv.at[2 + m]) for m in BOTH]
     p2 = to_across(r1buf.at[0], r2buf, x_send.at[0], x_recv.at[0])
     p3 = to_mate(r1buf.at[0], pao, x_send.at[1], x_recv.at[1])
@@ -320,14 +333,9 @@
         p1[m].wait()
         r1buf[m] = r1buf[m] + acc[m, mine, :]
 
-    def start_g(m):
-        gloc[m, 0:nown, :] = acc[m, 0:nown, :]
-        gloc[m, nown:, :] = gacc[m]
-        g1[m].start()
-
     def finish_g1(m):
         g1[m].wait()
-        gsum[m] = gloc[m] + gbuf1[m]
+        gsum[m] = gacc[m] + gbuf1[m]
         g2[m].start()
 
     def send_x(m):
@@ -346,11 +354,6 @@
         def _():
             x_own[m][0].wait_recv()
             x_peer[m][0].wait_recv()
-
-    def sums_a():
-        finish_g1(0)
-        add_half(0)
-        p2.start()
 
     def begin_chain():
         wait_x(0)
@@ -370,10 +373,6 @@
                 top_far[m][1].wait_recv()
                 swap[m].start()
 
-    def finish_chain():
-        chain_final(col, st, outs)
-        top_rows()
-
     def last_sums_a():
         p2.wait()
         r1buf[0] = r1buf[0] + r2buf[...]
@@ -381,10 +380,10 @@
         pam_out.start()
 
     last = trips - nchunk
-    begin = last - NP
-    hooks = [[(0, lambda: send_x(0))],
-             [(0, lambda: send_x(1)), (begin - 1, begin_chain), (last - 2, last_sums_a), (last - 1, finish_chain),
-              (last, lambda: start_g(1))]]
+    begin = 1
+    hooks = [[(0, lambda: send_x(0)), (last, lambda: finish_g1(0))],
+             [(begin - 1, begin_chain), (begin, lambda: send_x(1)), (last - 1, last_sums_a), (last - 1, top_rows),
+              (last, lambda: finish_g1(1))]]
 
     def products(m):
         def span(h, _):
@@ -402,8 +401,12 @@
 
             lax.fori_loop(0, SPAN // 512, build, 0)
             x = (xs[0], xs[1], xs[2])
-            r = dot6([xs[i, nown:, :] for i in range(3)], x, NT)
+            r = dot6(x, x, NT)
             gacc[m] = jnp.where(h == 0, r, gacc[m] + r)
+
+            @pl.when(h == spans - 1)
+            def _():
+                g1[m].start()
 
             def trip(j, _):
                 t = h * nchunk + j
@@ -419,21 +422,25 @@
                     def _():
                         c_copy(1, t + AHEAD - trips).start()
 
+                def piece(i):
+                    r = dot6(split3(cbuf[slot, i * PIECE:(i + 1) * PIECE, :]), (xs[0], xs[1], xs[2]), NT)
+                    d = pl.ds(pl.multiple_of(j * CHUNK + i * PIECE, PIECE), PIECE)
+                    acc[m, d, :] = jnp.where(h == 0, r, acc[m, d, :] + r)
+
                 def core_trip():
-                    r = dot6(split3(cbuf[slot]), (xs[0], xs[1], xs[2]), NT)
-                    d = pl.ds(pl.multiple_of(j * CHUNK, CHUNK), CHUNK)
-                    acc[m, d, :] = jnp.where(h == 0, r, acc[m, d, :] + r)
+                    for i in range(CHUNK // PIECE):
+                        piece(i)
 
                 if m == 0:
                     core_trip()
                 else:
-                    live = (t >= begin) & (t < last)
+                    live = (t >= begin) & (t < begin + NP)
 
                     @pl.when(live)
                     def _():
                         chain_cols(st)
                         core_trip()
-                        chain_update(t - begin, st, outs[4], outs[5])
+                        weave(chain_update(t - begin, st, outs[4], outs[5]), [])
 
                     pl.when(~live)(core_trip)
                 for at, hook in hooks[m]:
@@ -447,15 +454,15 @@
         lax.fori_loop(0, spans, span, 0)
 
     products(0)
-    start_g(0)
     p1[0].start()
     peer_out[0].start()
-    sums_a()
+    add_half(0)
+    p2.start()
     products(1)
     p1[1].start()
-    finish_g1(1)
     peer_out[1].start()
     wait_x(1)
+    chain_final(col, st, outs)
     add_half(1)
     pbm_out.start()
     g2[1].wait()
@@ -488,7 +495,7 @@
     ny = 2 * rows // SPAN
     shapes = [(own, rows)] * 2 + [(cols, N)] * 2 + [(half, N)] * 3 + [(N, N), (N, N)] + CHAIN_SHAPES
     scratch = CHAIN_SCRATCH + [(N, N), (2, own, rows), (2, own, rows)]
-    after = [(SLOTS, CHUNK, SPAN), (2, cols, N), (2, own, N), (2, half, N), (half, N)] + [pair] * 4
+    after = [(SLOTS, CHUNK, SPAN), (2, cols, N), pair, (2, half, N), (half, N)] + [pair] * 3
     return pl.pallas_call(
         exchange_kernel,
         in_specs=[hbm, hbm],
@@ -501,7 +508,7 @@
         compiler_params=pltpu.CompilerParams(vmem_limit_bytes=60 * 2**20, collective_id=0, has_side_effects=True))(ca, cb)
 
 
-def apply_update(ids, ct, peer, psum, poth, c1, small, before, nxt=None):
+def apply_update(ct, peer, psum, poth, c1, small, before, nxt=None, past=()):
     cols, rows = ct.shape
     nb = 512
     mb = 512
@@ -510,20 +517,21 @@
     steps = rows // nb
     rinvt, minv, upt, ptt, _, _, bad = small
     no = len(CHAIN_SHAPES)
-
-    def body(ids_ref, c_ref, x_ref, p_ref, q_ref, c1_ref, r_ref, m_ref, up_ref, pt_ref, bad_ref, before_ref, *refs):
-        if nxt is None:
-            o_ref, f_ref, z_ref, rc_ref = refs
-        else:
-            ins, (o_ref, f_ref), outs, (z_ref, rc_ref), st = refs[:2], refs[2:4], refs[4:4 + no], refs[4 + no:6 + no], refs[6 + no:]
+    extra = list(nxt or ()) + list(past)
+    ne = len(extra)
+
+    def body(c_ref, x_ref, p_ref, q_ref, c1_ref, r_ref, m_ref, up_ref, pt_ref, bad_ref, before_ref, *refs):
+        ins, (o_ref, f_ref) = refs[:ne], refs[ne:ne + 2]
+        outs, (z_ref, rc_ref, *st) = refs[ne + 2:len(refs) - ns], refs[len(refs) - ns:]
         i = pl.program_id(0)
-        top = ids_ref[0] == 0
+        row = lax.axis_index("row")
+        top = row == 0
 
         @pl.when(i == 0)
         def _():
             zero = jnp.zeros((1, 1), F32)
             for src, which in ((p_ref, 0), (q_ref, 1)):
-                base = pl.multiple_of((ids_ref[1] ^ which) * half, half)
+                base = pl.multiple_of((lax.rem(row, 2) ^ which) * half, half)
                 for j in range(half // mb):
                     s = slice(j * mb, (j + 1) * mb)
                     d = pl.ds(base + j * mb, mb)
@@ -534,53 +542,54 @@
                     zero = zero + jnp.sum(jnp.sum(z * 0.0, 0, keepdims=True), 1, keepdims=True)
             f_ref[...] = jnp.where(zero == 0.0, 0.0, 1.0) + bad_ref[...] + before_ref[...]
             if nxt is not None:
-                chain_init(ids_ref[2], *ins, st)
-
-        def products():
+                chain_init(lax.axis_index("col"), *ins[:2], st)
+                outs[4][0:N, :] = ins[2][...]
+                outs[4][2 * N:2 * N + NP, :] = ins[3][...]
+
+        def piece(j):
             x = jnp.concatenate([c_ref[0:own, :], x_ref[...]], 0)
-            o_ref[0:own, :] = hdot(up_ref[...], x)
-            o_ref[own:mb, :] = c_ref[own:mb, :] - hdot(z_ref[own:mb, :], x)
-            for j in range(1, cols // mb):
-                s = slice(j * mb, (j + 1) * mb)
-                o_ref[s, :] = c_ref[s, :] - hdot(z_ref[s, :], x)
-
+            lo = own if j == 0 else j * mb
+            if j == 0:
+                o_ref[0:own, :] = hdot(up_ref[...], x)
+            s = slice(lo, (j + 1) * mb)
+            o_ref[s, :] = c_ref[s, :] - hdot(z_ref[s, :], x)
+
+        pieces = [functools.partial(piece, j) for j in range(cols // mb)]
         if nxt is None:
-            products()
+            weave([], pieces)
         else:
             @pl.when(lax.rem(i, 2) == 0)
             def _():
                 chain_cols(st)
-                products()
+                weave([], pieces)
 
             @pl.when(lax.rem(i, 2) == 1)
             def _():
-                products()
-                chain_update(lax.div(i, 2), st, outs[4], outs[5])
+                weave(chain_update(lax.div(i, 2), st, outs[4].at[pl.ds(N, N), :], outs[4].at[pl.ds(2 * N + NP, NP), :]), pieces)
 
             @pl.when(i == steps - 1)
             def _():
-                chain_final(ids_ref[2], st, outs)
+                chain_final(lax.axis_index("col"), st, outs)
 
         @pl.when((i == 0) & top)
         def _():
             o_ref[0:own, 0:N] = pt_ref[...]
             o_ref[own:, 0:N] = rc_ref[own:, :]
 
-    blk2 = pl.BlockSpec((cols, nb), lambda i, r: (0, i))
-    fixed = lambda shape: pl.BlockSpec(shape, lambda i, r: (0, 0))
-    consts = [psum, poth, c1, rinvt, minv, upt, ptt, bad, before] + list(nxt or [])
-    more = CHAIN_SHAPES if nxt is not None else []
+    blk2 = pl.BlockSpec((cols, nb), lambda i: (0, i))
+    fixed = lambda shape: pl.BlockSpec(shape, lambda i: (0, 0))
+    consts = [psum, poth, c1, rinvt, minv, upt, ptt, bad, before] + extra
+    more = CHAIN_SHAPES[:4] + [(2 * (N + NP), W)] + CHAIN_SHAPES[5:] if nxt is not None else []
     scratch = [(cols, N), (cols, N)] + (CHAIN_SCRATCH if nxt is not None else [])
+    ns = len(scratch)
     return pl.pallas_call(
-        body,
-        grid_spec=pltpu.PrefetchScalarGridSpec(
-            num_scalar_prefetch=1, grid=(steps,),
-            in_specs=[blk2, pl.BlockSpec((own, nb), lambda i, r: (0, i))] + [fixed(a.shape) for a in consts],
-            out_specs=[blk2, fixed((8, 128))] + [fixed(s) for s in more],
-            scratch_shapes=[pltpu.VMEM(s, F32) for s in scratch]),
-        out_shape=[jax.ShapeDtypeStruct(s, F32) for s in [(cols, rows), (8, 128)] + more],
-        cost_estimate=pl.CostEstimate(flops=2 * 6 * cols * rows * N, bytes_accessed=8 * cols * rows, transcendentals=0),
-        compiler_params=pltpu.CompilerParams(vmem_limit_bytes=60 * 2**20))(ids, ct, peer, *consts)
+        body, grid=(steps,),
+        in_specs=[blk2, pl.BlockSpec((own, nb), lambda i: (0, i))] + [fixed(a.shape) for a in consts],
+        out_specs=[blk2, fixed(TILE)] + [fixed(s) for s in more],
+        scratch_shapes=[pltpu.VMEM(s, F32) for s in scratch],
+        out_shape=[jax.ShapeDtypeStruct(s, F32) for s in [(cols, rows), TILE] + more],
+        cost_estimate=pl.CostEstimate(flops=12 * cols * rows * N, bytes_accessed=8 * cols * rows, transcendentals=0),
+        compiler_params=pltpu.CompilerParams(vmem_limit_bytes=60 * 2**20))(ct, peer, *consts)
 
 
 R1 = [(0, 1), (1, 0), (2, 3), (3, 2)]
@@ -675,38 +684,39 @@
         local_rows, local_blocks, width = a_matrix.shape
         cols = local_blocks * width
         own = 2 * width
-        row_rank = lax.axis_index("row")
         col_rank = lax.axis_index("col")
-        core = row_rank % 2
         cts = [m.transpose(1, 2, 0).reshape(cols, local_rows) for m in (a_matrix, b_matrix)]
 
         pa, pb, c1a, c1b, pam, pao, pbm, g, x1, *first = exchange(*cts, own)
         across = lax.ppermute(pbm, "row", R2)
-        ids = jnp.stack([row_rank, core, col_rank]).astype(jnp.int32)
-        out_a, bad_a, *second = apply_update(ids, cts[0], pa, pam, pao, c1a, first, jnp.zeros(TILE, F32), (g, x1))
+        out_a, bad_a, *second = apply_update(cts[0], pa, pam, pao, c1a, first, first[6], (g, x1), (first[4], first[5]))
         across, bad_a = lax.optimization_barrier((across, bad_a))
         pbm = pbm + across
         pbo = lax.ppermute(pbm, "row", R1)
-        tt = jnp.concatenate([s[i] for s in (first, second) for i in (4, 5)], 0)
-        tt = jnp.where(col_rank == 0, tt, lax.ppermute(tt, "col", [(0, 1)]))
-        out_b, bad = apply_update(ids, cts[1], pb, pbm, pbo, c1b, second, bad_a)
-        bad = bad + lax.ppermute(bad, "col", CY)
-        carry = [bad]
+        small = lax.ppermute(second[4], "col", [(0, 1)])
+        out_b, bad = apply_update(cts[1], pb, pbm, pbo, c1b, second, bad_a)
+        small, bad = lax.optimization_barrier((small, bad))
+        small = jnp.where(col_rank == 0, second[4], small)
+        carry = (bad, lax.ppermute(bad, "col", CY), small, out_a, out_b)
+
+        def redo(state):
+            def one(i, done):
+                st, taus, tfs = factor_columns(jnp.where(i == 0, a_matrix, b_matrix))
+                new = (st.transpose(1, 2, 0).reshape(cols, local_rows), jnp.concatenate([tfs, taus.reshape(PANELS, width)], 0))
+                return tuple(jnp.where(i == k, n, d) for k, pair in enumerate((done[:2], done[2:])) for n, d in zip(new, pair))
+
+            blank = jnp.zeros((N + PANELS, width), F32)
+            st_a, tt_a, st_b, tt_b = lax.fori_loop(0, 2, one, (state[3], blank, state[4], blank))
+            tt = row_major(jnp.concatenate([tt_a[:N], tt_b[:N], tt_a[N:], tt_b[N:]], 0))
+            return jnp.zeros(TILE, F32), jnp.zeros(TILE, F32), tt, st_a, st_b
+
+        _, _, tt, out_a, out_b = lax.while_loop(lambda s: jnp.max(s[0] + s[1]) > 0.5, redo, carry)
+        back = lambda x: x.reshape(local_blocks, width, local_rows).transpose(2, 0, 1)
+        tail = []
         for i, out in enumerate((out_a, out_b)):
-            at = i * (N + NP)
-            carry += [out, tt[at + N:at + N + NP], tt[at:at + N]]
-
-        def redo(state):
-            new = [jnp.zeros(TILE, F32)]
-            for m in (a_matrix, b_matrix):
-                st, taus, tfs = factor_columns(m)
-                new += [st.transpose(1, 2, 0).reshape(cols, local_rows), row_major(taus.reshape(NP, W)), row_major(tfs)]
-            return tuple(new)
-
-        res = lax.while_loop(lambda s: s[0][0, 0] > 0.5, redo, tuple(carry))
-        back = lambda x: x.reshape(local_blocks, width, local_rows).transpose(2, 0, 1)
-        stack = lambda t: t.reshape(PANELS, width, width)
-        return back(res[1]), res[2].reshape(N), stack(res[3]), back(res[4]), res[5].reshape(N), stack(res[6])
+            at = 2 * N + i * PANELS
+            tail += [back(out), tt[at:at + PANELS].reshape(N), tt[i * N:(i + 1) * N].reshape(PANELS, width, width)]
+        return tuple(tail)
 
     spec_mat = P(("batch", "row"), "col", None)
     spec_out = (spec_mat, P("batch"), P("batch", None, None))

time: 241 us -> 221 us (0.917)
  Pallas kernels: 211 us -> 202 us
  waiting for transfers between devices: 7.02 us -> 2.18 us
    pallas_call x1, Pallas kernels: 120 us -> 113 us  [exchange(): pl.pallas_call(exchange_kernel, in_specs=[hbm, hbm], out_specs=[hbm] * 7...]
    ppermute x2, waiting for transfers between devices: 7.01 us -> 2.18 us  [the longest x1 2.17 us: factor_both(): carry = (bad, lax.ppermute(bad, 'col', CY), small, out_a, out_b)]
  transfers between devices with their start and end apart: 4 -> 4, of which waited for: 2 -> 1; matrix products, arithmetic and copies ran while one was open for 2% -> 0% of each run, Pallas kernels for 21% -> 41%
where the time goes in v2:
time: 221 us; the launch traced here: 218 us
  Pallas kernels  202 us (91%)
  local copies, waits for them, and re-layouts  5.31 us (2%)
  starting transfers between devices  4.8 us (2%)
    pallas_call x1, Pallas kernels, exchange(): pl.pallas_call(exchange_kernel, in_specs=[hbm, hbm], out_specs=[hbm] * 7...  113 us
    pallas_call x2, Pallas kernels, apply_update(): pl.pallas_call(body, grid=(steps,), in_specs=[blk2, pl.BlockSpec((own, nb...  89.1 us
  transfers between devices with their start and end apart: 4, of which 1 were waited for; matrix products, arithmetic and copies ran while one was open for 0% of the time, Pallas kernels for 41%

profile of v2, /device:TPU:0, one launch (start us, length us, event | category | flops | bytes accessed | tf_op | source)
XLA Modules:
  0.0 218.0 jit_solution(12774312823291003723)
XLA Ops:
  0.6 112.6 %shard_map.73 = (f32[128,4096]{1,0:T(8,128)}, f32[128,4096]{1,0:T(8,128)}, f32[2048,256]{1,0:T(8,128)}, f32[2048,256]{1,0:T(8,128)}, f32[1024,256]{1,0:T(8,128)}...) custom-call(f32[2048,4096]{1,0:T(8,128)} %bitcast.142, ...), custom_call_target="tpu_custom_call" | custom-call | flops 51539607552 | bytes 67108864 | tf_op jit(solution)/shard_map/pallas_call | solution.py:499
  113.2 1.0 collective-permute-start.9
  114.2 0.0 copy-start.1
  114.2 49.3 %shard_map.74 = (f32[2048,4096]{1,0:T(8,128)}, f32[8,128]{1,0:T(8,128)}, f32[256,256]{1,0:T(8,128)}, f32[256,256]{1,0:T(8,128)}, f32[128,256]{1,0:T(8,128)}, /*i...) custom-call(f32[2048,4096]{1,0:T(8,128)} %bitcast.143, ...), custom_call_target="tpu_custom_call" | custom-call | flops 25769803776 | bytes 67108864 | tf_op jit(solution)/shard_map/pallas_call | solution.py:585
  163.5 0.0 collective-permute-done.9
  163.5 0.0 copy-done.1
  163.5 0.1 add.292.p_ref
  163.7 0.0 copy-start.2
  163.7 0.0 collective-permute-start.10
  163.7 3.1 %collective-permute-start.8 = (f32[520,64]{1,0:T(8,128)}, f32[520,64]{1,0:T(8,128)S(1)}, u32[]{:S(2)}, u32[]{:S(2)}) collective-permute-start(f32[520,64]{1,0:T(8,128)} %get-tuple-element.996), channel_id=1, source_target_pairs={{0,4},{1,5},{2,6},{3,7}} | collective-permute-start | bytes 399368 | tf_op jit(solution)/shard_map/ppermute | solution.py:696
  166.8 0.0 collective-permute-done.10.q_ref
  166.8 0.0 copy-start.6
  166.8 0.0 copy-done.2
  166.8 1.0 copy-done.6
  167.8 0.0 copy-start.3
  167.8 39.8 %shard_map.75 = (f32[2048,4096]{1,0:T(8,128)}, f32[8,128]{1,0:T(8,128)S(1)}) custom-call(f32[2048,4096]{1,0:T(8,128)} %bitcast.141, f32[128,4096]{1,0:T(8,128)} %get-tuple-element.997.x_ref, f32[1024,256]{1,0:T(8,128)} %copy-done.2, f32[1024,256]{1,0:T(8,128)} %copy-done.6, f32[2048,256]{1,0:T(8,128)} %get-tuple-element.1001.c1_ref, ...), custom_call_target="tpu_custom_call" | custom-call | flops 25769803776 | bytes 67108864 | tf_op jit(solution)/shard_map/pallas_call | solution.py:585
  207.7 0.0 copy-start.4
  207.7 0.0 collective-permute-done.8
  207.7 0.7 collective-permute-start.11
  208.4 0.0 copy-done.3
  208.4 0.7 broadcast_select_fusion.2
  209.1 2.2 collective-permute-done.11
  211.3 0.0 copy-start.5
  211.3 0.0 copy-done.4
  211.3 0.6 copy-done.5
  211.9 2.0 while.209
  211.9 1.3 add_reduce_fusion.1
  213.8 1.7 fusion.41
  215.5 0.8 fusion.42
  216.3 0.6 reshape.158
  216.9 0.6 reshape.161
Async XLA Ops:
  113.2 50.3 %collective-permute-start.9 = (f32[1024,256]{1,0:T(8,128)}, f32[1024,256]{1,0:T(8,128)S(1)}, u32[]{:S(2)}, u32[]{:S(2)}) collective-permute-start(f32[1024,256]{1,0:T(8,128)} %get-tuple-element.998), channel_id=1, source_target_pairs={{0,2},{2,0},{1,3},{3,1},{4,6},{6,4},{5,7},{7,5}} | collective-permute-start | bytes 3145736 | tf_op jit(solution)/shard_map/ppermute | solution.py:691
  114.2 49.3 %copy-start.1 = (f32[1024,256]{1,0:T(8,128)S(1)}, f32[1024,256]{1,0:T(8,128)}, u32[]{:S(2)}) copy-start(f32[1024,256]{1,0:T(8,128)} %get-tuple-element.998) | copy-start | bytes 3145732
  163.7 3.2 %copy-start.2 = (f32[1024,256]{1,0:T(8,128)}, f32[1024,256]{1,0:T(8,128)S(1)}, u32[]{:S(2)}) copy-start(f32[1024,256]{1,0:T(8,128)S(1)} %add.292.p_ref) | copy-start | bytes 3145732
  163.7 3.1 %collective-permute-start.10 = (f32[1024,256]{1,0:T(8,128)S(1)}, f32[1024,256]{1,0:T(8,128)S(1)}, u32[]{:S(2)}, u32[]{:S(2)}) collective-permute-start(f32[1024,256]{1,0:T(8,128)S(1)} %add.292.p_ref), channel_id=1, source_target_pairs={{0,1},{1,0},{2,3},{3,2},{4,5},{5,4},{6,7},{7,6}} | collective-permute-start | bytes 3145736 | tf_op jit(solution)/shard_map/ppermute | solution.py:695
  163.7 43.9 %collective-permute-start.8 = (f32[520,64]{1,0:T(8,128)}, f32[520,64]{1,0:T(8,128)S(1)}, u32[]{:S(2)}, u32[]{:S(2)}) collective-permute-start(f32[520,64]{1,0:T(8,128)} %get-tuple-element.996), channel_id=1, source_target_pairs={{0,4},{1,5},{2,6},{3,7}} | collective-permute-start | bytes 399368 | tf_op jit(solution)/shard_map/ppermute | solution.py:696
  166.8 1.0 copy-start.6
  167.8 40.6 %copy-start.3 = (f32[520,64]{1,0:T(8,128)S(1)}, f32[520,64]{1,0:T(8,128)}, u32[]{:S(2)}) copy-start(f32[520,64]{1,0:T(8,128)} %get-tuple-element.996) | copy-start | bytes 399364
  207.7 3.6 %copy-start.4 = (f32[8,128]{1,0:T(8,128)}, f32[8,128]{1,0:T(8,128)S(1)}, u32[]{:S(2)}) copy-start(f32[8,128]{1,0:T(8,128)S(1)} %get-tuple-element.1855) | copy-start | bytes 12292
  207.7 3.6 %collective-permute-start.11 = (f32[8,128]{1,0:T(8,128)S(1)}, f32[8,128]{1,0:T(8,128)S(1)}, u32[]{:S(2)}, u32[]{:S(2)}) collective-permute-start(f32[8,128]{1,0:T(8,128)S(1)} %get-tuple-element.1855), channel_id=1, source_target_pairs={{0,4},{4,0},{1,5},{5,1},{2,6},{6,2},{3,7},{7,3}} | collective-permute-start | bytes 12296 | tf_op jit(solution)/shard_map/ppermute | solution.py:700
  211.3 0.6 copy-start.5

commit v3 on v2

--- a/solution.py
+++ b/solution.py
@@ -20,6 +20,8 @@
 
 
 BOTH = (0, 1)
+total = functools.partial(jnp.sum, keepdims=True)
+peak = functools.partial(jnp.max, keepdims=True)
 TILE = (8, 128)
 
 
@@ -120,7 +122,7 @@
     return jnp.concatenate([x[:, W:N], x[:, :W], x[:, N:]], 1)
 
 
-CHAIN_SCRATCH = [(N, 2 * N), (N, 2 * N), (N, N), (4, W, W), (8, N), (8, W)]
+CHAIN_SCRATCH = [(N, 2 * N), (N, 2 * N), (N, N), (NP, 4, W, W), (8, N), (NP, W)]
 CHAIN_SHAPES = [(N, N), (N, N), (2 * W, N), (2 * W, N), (N, W), (NP, W), TILE]
 
 
@@ -139,39 +141,33 @@
     ys[:, :N] = ls[...].T
     ys[:, N:] = eye
     dg = jnp.where(ri == ci, hs[:, :N], 0.0)
-    norm[...] = jnp.broadcast_to(jnp.sqrt(jnp.sum(dg, 0, keepdims=True)), (8, N))
-
-
-def chain_cols(st):
+    norm[...] = jnp.broadcast_to(jnp.sqrt(total(dg, 0)), (8, N))
+
+
+def chain_cols(p, st):
     hs, ys, _, fac, _, tv = st
     e, l, u, w, tau = diag_factor([(hs[0:W, 0:W], ys[0:W, 0:W])])[0]
     for i, x in enumerate((e, l, u, w)):
-        fac[i] = x
-    tv[...] = jnp.broadcast_to(tau, (8, W))
-
-
-def chain_update(p, st, tfac, tau):
-    hs, ys, ls, fac, _, tv = st
-    r64 = rows_of((W, W))
-    c64 = lanes_of((W, W))
+        fac[p, i] = x
+    tv[pl.ds(p, 1), :] = tau
+
+
+def chain_update(p, st):
+    hs, ys, ls, fac, _, _ = st
     rw = rows_of((W, 2 * N))
     cw = lanes_of((W, 2 * N))
     rl = rows_of((N - W, W))
     live = N - p * W
-    e, l, u, w = fac[0], fac[1], fac[2], fac[3]
-    d = pl.ds(pl.multiple_of(p * W, W), W)
+    e, l, w = fac[p, 0], fac[p, 1], fac[p, 3]
     rall = hdot(e, hs[0:W, :])
     rall = jnp.where((cw >= N) | ((cw >= rw) & (cw < live)), rall, 0.0)
-    ue, uw, wl = hdot(u, e, NT), hdot(u, w), hdot(w, l)
+    wl = hdot(w, l)
     yield
     yc = ys[W:, 0:W]
     nrow = hdot(w, ys[0:W, :] - jnp.where(cw < N, rall, 0.0))
     hnew = hs[W:, :] - hdot(rall[:, W:N], rall, TN)
     hs[0:N - W, :] = turn(hnew)
     hs[N - W:, :] = turn(rall)
-    t = -hdot(ue, uw, NT)
-    tfac[d, :] = jnp.where(c64 > r64, t, jnp.where(c64 == r64, jnp.broadcast_to(tv[0:1, :], (W, W)), 0.0))
-    tau[pl.ds(p, 1), :] = tv[0:1, :]
     lnew = jnp.where(rl < live - W, hdot(yc, wl), 0.0)
     rest = ls[W:, W:]
     first = ls[0:W, W:]
@@ -195,15 +191,22 @@
 
 
 def chain_final(col, st, outs):
-    hs, ys, ls, _, norm, _ = st
-    rinvt, minv, upt, ptt, _, _, bad = outs
+    hs, ys, ls, fac, norm, tv = st
+    rinvt, minv, upt, ptt, tfac, tau, bad = outs
+    r64 = rows_of((W, W))
+    c64 = lanes_of((W, W))
+    tau[...] = tv[...]
+    for p in range(NP):
+        e, _, u, w = [fac[p, i] for i in range(4)]
+        t = -hdot(hdot(u, e, NT), hdot(u, w), NT)
+        tfac[blk(p), :] = jnp.where(c64 > r64, t, jnp.where(c64 == r64, jnp.broadcast_to(tv[p:p + 1, :], (W, W)), 0.0))
     ri = rows_of((N, N))
     ci = lanes_of((N, N))
     rt, mi = hs[:, N:], ys[:, N:]
     g = norm[0:1, :]
-    c1 = jnp.max(jnp.sum(jnp.abs(rt) * g, 1, keepdims=True), keepdims=True)
-    c2 = jnp.max(hdot(g, jnp.abs(mi)), keepdims=True)
-    good = (c1 <= AMPLIFY) & (c2 <= AMPLIFY) & (jnp.min(g, keepdims=True) >= 1 / HUGE) & (jnp.max(g, keepdims=True) <= HUGE)
+    c1 = peak(total(jnp.abs(rt) * g, 1))
+    c2 = peak(hdot(g, jnp.abs(mi)))
+    good = (c1 <= AMPLIFY) & (c2 <= AMPLIFY) & (-peak(-g) >= 1 / HUGE) & (peak(g) <= HUGE)
     bad[...] = jnp.broadcast_to(jnp.where(good, 0.0, 1.0), TILE)
     pt = jnp.where(ri > ci, ls[...], hs[:, :N]).T
     ut = lax.dot_general(ls[...], mi, (((0,), (1,)), ((), ())), precision=HI, preferred_element_type=F32)
@@ -222,6 +225,10 @@
                     upt[blk(i), blk(i2)] = ys[blk(b), blk(b2)]
 
 
+SPLITS = range(3)
+loop = functools.partial(lax.fori_loop, 0)
+
+
 def split3(x):
     h = x.astype(BF)
     r = x - h.astype(F32)
@@ -234,8 +241,9 @@
     return (((d(2, 0) + d(0, 2)) + d(1, 1)) + (d(1, 0) + d(0, 1))) + d(0, 0)
 
 
-CHUNK = 1024
-PIECE = 512
+CHUNK = 960
+PIECE = 480
+HALF = 512
 SPAN = 1024
 SLOTS = 3
 AHEAD = SLOTS - 1
@@ -244,7 +252,7 @@
 def exchange_kernel(ca, cb, peer_a, peer_b, c1a, c1b, pam, pao, pbm, g_out, x1b, *refs):
     outs, refs = refs[:len(CHAIN_SHAPES)], refs[len(CHAIN_SHAPES):]
     st, refs = refs[:len(CHAIN_SCRATCH)], refs[len(CHAIN_SCRATCH):]
-    (x1a, peer, own, xs, cbuf, acc, gacc, r1buf, r2buf, gbuf1, gsum, gbuf2,
+    (x1a, peer, own, xo, xs, cbuf, acc, gacc, r1buf, r2buf, gbuf1, gsum, gbuf2, gfull,
      c_sem, own_sem, out_sem, y_send, y_recv, top_send, top_recv, swap_send, swap_recv,
      g_send, g_recv, p_send, p_recv, x_send, x_recv) = refs
     cts, x1 = (ca, cb), (x1a, x1b)
@@ -257,7 +265,7 @@
     cols, rows = ca.shape
     half = cols // 2
     nown = peer.shape[1]
-    nchunk = cols // CHUNK
+    nchunk = (cols - nown) // CHUNK
     spans = rows // SPAN
     trips = nchunk * spans
 
@@ -272,7 +280,7 @@
         slot = lax.rem(m * trips + t, SLOTS)
         h, j = lax.div(t, nchunk), lax.rem(t, nchunk)
         return pltpu.make_async_copy(
-            cts[m].at[pl.ds(pl.multiple_of(j * CHUNK, CHUNK), CHUNK), pl.ds(pl.multiple_of(h * SPAN, SPAN), SPAN)],
+            cts[m].at[pl.ds(pl.multiple_of(nown + j * CHUNK, 64), CHUNK), pl.ds(pl.multiple_of(h * SPAN, SPAN), SPAN)],
             cbuf.at[slot], c_sem.at[slot])
 
     first = pl.ds(0, nown)
@@ -283,6 +291,20 @@
         s = pl.ds(pl.multiple_of(h * SPAN, SPAN), SPAN)
         i = m * spans + h
         return remote(cts[m].at[first, s], peer.at[m, :, s], y_send.at[i], y_recv.at[i], col=1 - col)
+
+    def half_slot(u):
+        return lax.rem(2 * trips - nchunk + u, SLOTS)
+
+    def c_half(u):
+        q, j = lax.div(u, nchunk), lax.rem(u, nchunk)
+        return pltpu.make_async_copy(
+            cb.at[pl.ds(pl.multiple_of(nown + j * CHUNK, 64), CHUNK), pl.ds(pl.multiple_of(rows - SPAN + q * HALF, HALF), HALF)],
+            cbuf.at[half_slot(u), :, pl.ds(0, HALF)], c_sem.at[half_slot(u)])
+
+    def y_half(q):
+        s = pl.ds(pl.multiple_of(rows - SPAN + q * HALF, HALF), HALF)
+        i = 2 * spans - 1 + q
+        return remote(cb.at[first, s], peer.at[1, :, s], y_send.at[i], y_recv.at[i], col=1 - col)
 
     own_copies = [pltpu.make_async_copy(cts[m].at[first, :], own.at[m], own_sem.at[m]) for m in BOTH]
     for o in own_copies:
@@ -290,22 +312,24 @@
     for t in range(AHEAD):
         c_copy(0, t).start()
 
+    for m in BOTH:
+        acc[m, 0:nown, :] = jnp.zeros((nown, N), F32)
     barrier = pltpu.get_barrier_semaphore()
     for where in (dict(row=mate), dict(row=across), dict(row=diag), dict(col=1 - col)):
         pl.semaphore_signal(barrier, device_id=where, device_id_type=pl.DeviceIdType.MESH)
     pl.semaphore_wait(barrier, 4)
 
-    for m in BOTH:
-        for h in range(spans):
-            y_copy(m, h).start()
+    ys = [y_copy(m, h) for m in BOTH for h in range(spans - m)] + [y_half(q) for q in BOTH]
+    for y in ys:
+        y.start()
 
     tops = (c1a, c1b)
     lows = [pl.ds(0, half), pl.ds(half, half)]
     x_local = [pltpu.make_async_copy(cts[m].at[first, lanes], x1[m].at[first, :], own_sem.at[2 + m]) for m in BOTH]
     x_own = [[remote(cts[m].at[first, lanes], x1[m].at[first, :], top_send.at[m, k], top_recv.at[m], row=k + 1)
-              for k in range(3)] for m in BOTH]
+              for k in SPLITS] for m in BOTH]
     x_peer = [[remote(peer.at[m, :, lanes], x1[m].at[second, :], top_send.at[2 + m, k], top_recv.at[2 + m], row=k + 1)
-               for k in range(3)] for m in BOTH]
+               for k in SPLITS] for m in BOTH]
     top_far = [[remote(cts[m].at[:, lanes], tops[m], top_send.at[4 + m, 0], top_recv.at[4 + m], row=1)]
                + [remote(cts[m].at[lows[k], lanes], tops[m].at[lows[k], :], top_send.at[4 + m, 1 + k], top_recv.at[4 + m], row=2 + k)
                   for k in BOTH] for m in BOTH]
@@ -319,15 +343,17 @@
 
     mine = pl.ds(pl.multiple_of(core * half, half), half)
     others = pl.ds(pl.multiple_of((1 - core) * half, half), half)
+    g_mine = pl.ds(pl.multiple_of(core * nown, nown), nown)
+    g_theirs = pl.ds(pl.multiple_of((1 - core) * nown, nown), nown)
     p1 = [to_mate(acc.at[m, others, :], r1buf.at[m], p_send.at[m], p_recv.at[m]) for m in BOTH]
-    g1 = [to_mate(gacc.at[m], gbuf1.at[m], g_send.at[m], g_recv.at[m]) for m in BOTH]
+    g1 = [to_mate(gacc.at[m, g_theirs, :], gbuf1.at[m], g_send.at[m], g_recv.at[m]) for m in BOTH]
     g2 = [to_across(gsum.at[m], gbuf2.at[m], g_send.at[2 + m], g_recv.at[2 + m]) for m in BOTH]
+    g3 = [to_mate(full.at[g_mine, :], full.at[g_mine, :], g_send.at[4 + m], g_recv.at[4 + m]) for m, full in enumerate((gfull, g_out))]
     p2 = to_across(r1buf.at[0], r2buf, x_send.at[0], x_recv.at[0])
     p3 = to_mate(r1buf.at[0], pao, x_send.at[1], x_recv.at[1])
     swap = [to_mate(tops[m].at[mine, :], tops[m].at[mine, :], swap_send.at[m], swap_recv.at[m]) for m in BOTH]
     peer_out = [pltpu.make_async_copy(peer.at[m], (peer_a, peer_b)[m], out_sem.at[m]) for m in BOTH]
     pam_out = pltpu.make_async_copy(r1buf.at[0], pam, out_sem.at[2])
-    pbm_out = pltpu.make_async_copy(r1buf.at[1], pbm, out_sem.at[3])
 
     def add_half(m):
         p1[m].wait()
@@ -335,8 +361,13 @@
 
     def finish_g1(m):
         g1[m].wait()
-        gsum[m] = gacc[m] + gbuf1[m]
+        gsum[m] = gacc[m, g_mine, :] + gbuf1[m]
         g2[m].start()
+
+    def finish_g2(m, full):
+        g2[m].wait()
+        full[g_mine, :] = gsum[m] + gbuf2[m]
+        g3[m].start()
 
     def send_x(m):
         @pl.when(row == 0)
@@ -357,9 +388,8 @@
 
     def begin_chain():
         wait_x(0)
-        g2[0].wait()
-        gsum[0] = gsum[0] + gbuf2[0]
-        chain_init(col, gsum.at[0], x1a, st)
+        g3[0].wait()
+        chain_init(col, gfull, x1a, st)
 
     def top_rows():
         @pl.when(row == 1)
@@ -382,91 +412,133 @@
     last = trips - nchunk
     begin = 1
     hooks = [[(0, lambda: send_x(0)), (last, lambda: finish_g1(0))],
-             [(begin - 1, begin_chain), (begin, lambda: send_x(1)), (last - 1, last_sums_a), (last - 1, top_rows),
-              (last, lambda: finish_g1(1))]]
-
-    def products(m):
+             [(begin - 1, begin_chain), (begin, lambda: send_x(1)), (last - 1, last_sums_a), (last - 1, top_rows)]]
+
+    def split_own(m):
+        def build(q, _):
+            s = pl.ds(pl.multiple_of(q * HALF, HALF), HALF)
+            for i, part in enumerate(split3(own[m, :, s])):
+                xo[m, i, :, s] = part
+            return 0
+
+        own_copies[m].wait()
+        loop(rows // HALF, build, 0)
+
+    def panel(m, s0, width):
+        return [jnp.concatenate([xo[m, i, :, pl.ds(s0, width)], xs[i, :, 0:width]], 0) for i in SPLITS]
+
+    def head(m, s0, width):
+        for q in range(width // HALF):
+            d = slice(q * HALF, (q + 1) * HALF)
+            for i, part in enumerate(split3(peer[m, :, pl.ds(s0 + q * HALF, HALF)])):
+                xs[i, :, d] = part
+        x = panel(m, s0, width)
+        return dot6(x, x, NT)
+
+    def trip(m, j, slot, s0, width, fresh):
+        x = panel(m, s0, width)
+        for i in range(CHUNK // PIECE):
+            r = dot6(split3(cbuf[slot, i * PIECE:(i + 1) * PIECE, 0:width]), x, NT)
+            d = pl.ds(pl.multiple_of(nown + j * CHUNK + i * PIECE, 32), PIECE)
+            acc[m, d, :] = jnp.where(fresh, r, acc[m, d, :] + r)
+
+    def products(m, count):
         def span(h, _):
             y_copy(m, h).wait_recv()
             s0 = pl.multiple_of(h * SPAN, SPAN)
-
-            def build(q, _):
-                d = pl.ds(pl.multiple_of(q * 512, 512), 512)
-                s = pl.ds(pl.multiple_of(s0 + q * 512, 512), 512)
-                for i, part in enumerate(split3(own[m, :, s])):
-                    xs[i, 0:nown, d] = part
-                for i, part in enumerate(split3(peer[m, :, s])):
-                    xs[i, nown:, d] = part
-                return 0
-
-            lax.fori_loop(0, SPAN // 512, build, 0)
-            x = (xs[0], xs[1], xs[2])
-            r = dot6(x, x, NT)
+            r = head(m, s0, SPAN)
             gacc[m] = jnp.where(h == 0, r, gacc[m] + r)
 
-            @pl.when(h == spans - 1)
-            def _():
-                g1[m].start()
-
-            def trip(j, _):
+            if m == 0:
+                @pl.when(h == spans - 1)
+                def _():
+                    g1[0].start()
+
+            def step(j, _):
                 t = h * nchunk + j
                 slot = lax.rem(m * trips + t, SLOTS)
                 c_copy(m, t).wait()
-
-                @pl.when(t + AHEAD < trips)
+                ahead = t + AHEAD - count * nchunk
+
+                @pl.when(ahead < 0)
                 def _():
                     c_copy(m, t + AHEAD).start()
 
+                @pl.when(ahead >= 0)
+                def _():
+                    (c_copy(1, ahead) if m == 0 else c_half(ahead)).start()
+
+                run = functools.partial(trip, m, j, slot, s0, SPAN, h == 0)
                 if m == 0:
-                    @pl.when(t + AHEAD >= trips)
-                    def _():
-                        c_copy(1, t + AHEAD - trips).start()
-
-                def piece(i):
-                    r = dot6(split3(cbuf[slot, i * PIECE:(i + 1) * PIECE, :]), (xs[0], xs[1], xs[2]), NT)
-                    d = pl.ds(pl.multiple_of(j * CHUNK + i * PIECE, PIECE), PIECE)
-                    acc[m, d, :] = jnp.where(h == 0, r, acc[m, d, :] + r)
-
-                def core_trip():
-                    for i in range(CHUNK // PIECE):
-                        piece(i)
-
-                if m == 0:
-                    core_trip()
+                    run()
                 else:
                     live = (t >= begin) & (t < begin + NP)
 
                     @pl.when(live)
                     def _():
-                        chain_cols(st)
-                        core_trip()
-                        weave(chain_update(t - begin, st, outs[4], outs[5]), [])
-
-                    pl.when(~live)(core_trip)
+                        chain_cols(t - begin, st)
+                        run()
+                        weave(chain_update(t - begin, st), [])
+
+                    pl.when(~live)(run)
                 for at, hook in hooks[m]:
                     pl.when(t == at)(hook)
                 return 0
 
-            lax.fori_loop(0, nchunk, trip, 0)
+            loop(nchunk, step, 0)
             return 0
 
-        own_copies[m].wait()
-        lax.fori_loop(0, spans, span, 0)
-
-    products(0)
+        loop(count, span, 0)
+
+    def last_span():
+        def span(q, _):
+            y_half(q).wait_recv()
+            s0 = pl.multiple_of(rows - SPAN + q * HALF, HALF)
+            gacc[1] = gacc[1] + head(1, s0, HALF)
+
+            @pl.when(q == 1)
+            def _():
+                g1[1].start()
+
+            def step(j, _):
+                u = q * nchunk + j
+                c_half(u).wait()
+
+                @pl.when(u + AHEAD < 2 * nchunk)
+                def _():
+                    c_half(u + AHEAD).start()
+
+                trip(1, j, half_slot(u), s0, HALF, False)
+
+                @pl.when(u == nchunk)
+                def _():
+                    finish_g1(1)
+
+                return 0
+
+            loop(nchunk, step, 0)
+            return 0
+
+        loop(2, span, 0)
+
+    for m in BOTH:
+        split_own(m)
+    products(0, spans)
     p1[0].start()
     peer_out[0].start()
     add_half(0)
     p2.start()
-    products(1)
+    finish_g2(0, gfull)
+    products(1, spans - 1)
+    last_span()
     p1[1].start()
     peer_out[1].start()
     wait_x(1)
     chain_final(col, st, outs)
-    add_half(1)
-    pbm_out.start()
-    g2[1].wait()
-    g_out[...] = gsum[1] + gbuf2[1]
+    p1[1].wait()
+    pbm[...] = r1buf[1] + acc[1, mine, :]
+    finish_g2(1, g_out)
+    g3[1].wait()
 
     @pl.when(row == 0)
     def _():
@@ -478,11 +550,10 @@
         for m in BOTH:
             swap[m].wait()
 
-    for c in peer_out + [p3, pam_out, pbm_out]:
+    for c in peer_out + [p3, pam_out]:
         c.wait()
-    for m in BOTH:
-        for h in range(spans):
-            y_copy(m, h).wait_send()
+    for y in ys:
+        y.wait_send()
 
 
 def exchange(ca, cb, own):
@@ -492,18 +563,18 @@
     vm = pl.BlockSpec(memory_space=pltpu.VMEM)
     dma = pltpu.SemaphoreType.DMA
     pair = (2, N, N)
-    ny = 2 * rows // SPAN
+    ny = 2 * rows // SPAN + 1
     shapes = [(own, rows)] * 2 + [(cols, N)] * 2 + [(half, N)] * 3 + [(N, N), (N, N)] + CHAIN_SHAPES
     scratch = CHAIN_SCRATCH + [(N, N), (2, own, rows), (2, own, rows)]
-    after = [(SLOTS, CHUNK, SPAN), (2, cols, N), pair, (2, half, N), (half, N)] + [pair] * 3
+    after = [(SLOTS, CHUNK, SPAN), (2, cols, N), pair, (2, half, N), (half, N)] + [(2, own, N)] * 3 + [(N, N)]
     return pl.pallas_call(
         exchange_kernel,
         in_specs=[hbm, hbm],
-        out_specs=[hbm] * 7 + [vm] * (2 + len(CHAIN_SHAPES)),
+        out_specs=[hbm] * 6 + [vm] * (3 + len(CHAIN_SHAPES)),
         out_shape=[jax.ShapeDtypeStruct(s, F32) for s in shapes],
-        scratch_shapes=[pltpu.VMEM(s, F32) for s in scratch] + [pltpu.VMEM((3, 2 * own, SPAN), BF)]
+        scratch_shapes=[pltpu.VMEM(s, F32) for s in scratch] + [pltpu.VMEM((2, 3, own, rows), BF), pltpu.VMEM((3, own, SPAN), BF)]
         + [pltpu.VMEM(s, F32) for s in after]
-        + [dma(n) for n in ((SLOTS,), (4,), (4,), (ny,), (ny,), (6, 3), (6,), (2,), (2,), (4,), (4,), (2,), (2,), (2,), (2,))],
+        + [dma(n) for n in ((SLOTS,), (4,), (4,), (ny,), (ny,), (6, 3), (6,), (2,), (2,), (6,), (6,), (2,), (2,), (2,), (2,))],
         cost_estimate=pl.CostEstimate(flops=24 * cols * rows * N, bytes_accessed=8 * cols * rows, transcendentals=0),
         compiler_params=pltpu.CompilerParams(vmem_limit_bytes=60 * 2**20, collective_id=0, has_side_effects=True))(ca, cb)
 
@@ -530,7 +601,7 @@
         @pl.when(i == 0)
         def _():
             zero = jnp.zeros((1, 1), F32)
-            for src, which in ((p_ref, 0), (q_ref, 1)):
+            for which, src in enumerate((p_ref, q_ref)):
                 base = pl.multiple_of((lax.rem(row, 2) ^ which) * half, half)
                 for j in range(half // mb):
                     s = slice(j * mb, (j + 1) * mb)
@@ -539,7 +610,7 @@
                     z = hdot(jnp.where(top, c_ref[d, 0:N], c1_ref[d, :]) - rc, m_ref[...], NT)
                     rc_ref[d, :] = rc
                     z_ref[d, :] = z
-                    zero = zero + jnp.sum(jnp.sum(z * 0.0, 0, keepdims=True), 1, keepdims=True)
+                    zero = zero + total(total(z * 0.0, 0), 1)
             f_ref[...] = jnp.where(zero == 0.0, 0.0, 1.0) + bad_ref[...] + before_ref[...]
             if nxt is not None:
                 chain_init(lax.axis_index("col"), *ins[:2], st)
@@ -560,16 +631,17 @@
         else:
             @pl.when(lax.rem(i, 2) == 0)
             def _():
-                chain_cols(st)
+                chain_cols(lax.div(i, 2), st)
                 weave([], pieces)
 
             @pl.when(lax.rem(i, 2) == 1)
             def _():
-                weave(chain_update(lax.div(i, 2), st, outs[4].at[pl.ds(N, N), :], outs[4].at[pl.ds(2 * N + NP, NP), :]), pieces)
+                weave(chain_update(lax.div(i, 2), st), pieces)
 
             @pl.when(i == steps - 1)
             def _():
-                chain_final(lax.axis_index("col"), st, outs)
+                tts = (outs[4].at[pl.ds(N, N), :], outs[4].at[pl.ds(2 * N + NP, NP), :])
+                chain_final(lax.axis_index("col"), st, (*outs[:4], *tts, outs[6]))
 
         @pl.when((i == 0) & top)
         def _():
@@ -604,6 +676,10 @@
     return pl.pallas_call(body, out_shape=jax.ShapeDtypeStruct(x.shape, F32))(x)
 
 
+def pick(x, i, axis=0):
+    return lax.dynamic_slice_in_dim(x, i, 1, axis)
+
+
 def row_sum(x):
     x = x + lax.ppermute(x, "row", R1)
     return x + lax.ppermute(x, "row", R2)
@@ -622,18 +698,18 @@
         row_start = panel_idx * width
         local_idx = panel_idx // 2
         is_owner = col_rank == panel_idx % 2
-        panel_in = lax.dynamic_slice_in_dim(stored, local_idx, 1, axis=1)[:, 0, :]
+        panel_in = pick(stored, local_idx, 1)[:, 0, :]
 
         def column_step(col_idx, loop_state):
             work, tau_vec = loop_state
             diag_idx = row_start + col_idx
-            column = lax.dynamic_slice_in_dim(work, col_idx, 1, axis=1)[:, 0]
+            column = pick(work, col_idx, 1)[:, 0]
             below = jnp.where(row_ids >= diag_idx, column, 0.0)
             at_diag = (row_ids == diag_idx).astype(F32)
             summed = row_sum(edot("ar,rk->ak", jnp.stack([below, at_diag]), work))
             cross, diag_row = summed[0], summed[1]
-            pivot = lax.dynamic_slice_in_dim(diag_row, col_idx, 1)[0]
-            norm = jnp.sqrt(lax.dynamic_slice_in_dim(cross, col_idx, 1)[0])
+            pivot = pick(diag_row, col_idx)[0]
+            norm = jnp.sqrt(pick(cross, col_idx)[0])
             beta = -jnp.where(pivot >= 0, 1.0, -1.0) * norm
             tau = (beta - pivot) / beta
             denom = pivot - beta
@@ -641,42 +717,43 @@
             refl = jnp.where(row_ids > diag_idx, column / denom, 0.0) + at_diag
             work = work - tau * refl[:, None] * proj[None, :]
             new_col = jnp.where(row_ids < diag_idx, column, jnp.where(row_ids == diag_idx, beta, refl))
-            work = lax.dynamic_update_slice_in_dim(work, new_col[:, None], col_idx, axis=1)
-            return work, lax.dynamic_update_slice_in_dim(tau_vec, tau[None], col_idx, axis=0)
-
-        work, tau_vec = lax.fori_loop(0, width, column_step, (panel_in, jnp.zeros((width,), F32)))
+            work = lax.dynamic_update_slice_in_dim(work, new_col[:, None], col_idx, 1)
+            return work, lax.dynamic_update_slice_in_dim(tau_vec, tau[None], col_idx, 0)
+
+        work, tau_vec = loop(width, column_step, (panel_in, jnp.zeros((width,), F32)))
         diag_ids = row_start + col_ids[None, :]
         v_block = jnp.where(row_ids[:, None] == diag_ids, 1.0, jnp.where(row_ids[:, None] > diag_ids, work, 0.0))
+
         gram = row_sum(edot("ri,rj->ij", v_block, v_block))
 
         def t_step(col_idx, tf):
-            g = lax.dynamic_slice_in_dim(gram, col_idx, 1, axis=1)[:, 0]
+            g = pick(gram, col_idx, 1)[:, 0]
             g = jnp.where(col_ids < col_idx, g, 0.0)
-            tau_k = lax.dynamic_slice_in_dim(tau_vec, col_idx, 1)[0]
+            tau_k = pick(tau_vec, col_idx)[0]
             t_col = -tau_k * edot("ij,j->i", tf, g)
             t_col = jnp.where(col_ids == col_idx, tau_k, t_col)
-            return lax.dynamic_update_slice_in_dim(tf, t_col[:, None], col_idx, axis=1)
-
-        tf = lax.fori_loop(0, width, t_step, jnp.zeros((width, width), F32))
+            return lax.dynamic_update_slice_in_dim(tf, t_col[:, None], col_idx, 1)
+
+        tf = loop(width, t_step, jnp.zeros((width, width), F32))
         v_mine = jnp.where(is_owner, v_block, 0.0)
         t_mine = jnp.where(is_owner, tf, 0.0)
         v_block = v_mine + lax.ppermute(v_mine, "col", CY)
         tf = t_mine + lax.ppermute(t_mine, "col", CY)
 
         def block_step(b, stored):
-            blk = lax.dynamic_slice_in_dim(stored, b, 1, axis=1)[:, 0, :]
+            blk = pick(stored, b, 1)[:, 0, :]
             w = edot("ij,ik->jk", tf, row_sum(edot("ri,rk->ik", v_block, blk)))
             upd = blk - edot("ri,ik->rk", v_block, w)
             keep = b * 2 + col_rank > panel_idx
             mine = (b == local_idx) & is_owner
             new = jnp.where(keep, upd, jnp.where(mine, work, blk))
-            return lax.dynamic_update_slice_in_dim(stored, new[:, None, :], b, axis=1)
-
-        stored = lax.fori_loop(0, local_blocks, block_step, stored)
-        taus = lax.dynamic_update_slice_in_dim(taus, jnp.diagonal(tf), row_start, axis=0)
-        return stored, taus, lax.dynamic_update_slice_in_dim(tfs, tf, row_start, axis=0)
-
-    return lax.fori_loop(0, PANELS, panel_step, (stored, jnp.zeros((PANELS * width,), F32), jnp.zeros((PANELS * width, width), F32)))
+            return lax.dynamic_update_slice_in_dim(stored, new[:, None, :], b, 1)
+
+        stored = loop(local_blocks, block_step, stored)
+        taus = lax.dynamic_update_slice_in_dim(taus, jnp.diagonal(tf), row_start, 0)
+        return stored, taus, lax.dynamic_update_slice_in_dim(tfs, tf, row_start, 0)
+
+    return loop(PANELS, panel_step, (stored, jnp.zeros((PANELS * width,), F32), jnp.zeros((PANELS * width, width), F32)))
 
 
 def solution(mesh):
@@ -696,8 +773,12 @@
         small = lax.ppermute(second[4], "col", [(0, 1)])
         out_b, bad = apply_update(cts[1], pb, pbm, pbo, c1b, second, bad_a)
         small, bad = lax.optimization_barrier((small, bad))
-        small = jnp.where(col_rank == 0, second[4], small)
-        carry = (bad, lax.ppermute(bad, "col", CY), small, out_a, out_b)
+        tt = jnp.where(col_rank == 0, second[4], small)
+
+        def parts(tt):
+            return tt[:N], tt[N:2 * N], *(x.reshape(N) for x in jnp.split(tt[2 * N:], 2))
+
+        carry = (bad, lax.ppermute(bad, "col", CY), *parts(tt), out_a, out_b)
 
         def redo(state):
             def one(i, done):
@@ -706,17 +787,14 @@
                 return tuple(jnp.where(i == k, n, d) for k, pair in enumerate((done[:2], done[2:])) for n, d in zip(new, pair))
 
             blank = jnp.zeros((N + PANELS, width), F32)
-            st_a, tt_a, st_b, tt_b = lax.fori_loop(0, 2, one, (state[3], blank, state[4], blank))
+            st_a, tt_a, st_b, tt_b = loop(2, one, (state[6], blank, state[7], blank))
             tt = row_major(jnp.concatenate([tt_a[:N], tt_b[:N], tt_a[N:], tt_b[N:]], 0))
-            return jnp.zeros(TILE, F32), jnp.zeros(TILE, F32), tt, st_a, st_b
-
-        _, _, tt, out_a, out_b = lax.while_loop(lambda s: jnp.max(s[0] + s[1]) > 0.5, redo, carry)
+            return jnp.zeros(TILE, F32), jnp.zeros(TILE, F32), *(row_major(x) for x in parts(tt)), st_a, st_b
+
+        res = lax.while_loop(lambda s: jnp.max(s[0] + s[1]) > 0.5, redo, carry)
         back = lambda x: x.reshape(local_blocks, width, local_rows).transpose(2, 0, 1)
-        tail = []
-        for i, out in enumerate((out_a, out_b)):
-            at = 2 * N + i * PANELS
-            tail += [back(out), tt[at:at + PANELS].reshape(N), tt[i * N:(i + 1) * N].reshape(PANELS, width, width)]
-        return tuple(tail)
+        stack = lambda x: x.reshape(PANELS, width, width)
+        return back(res[6]), res[4], stack(res[2]), back(res[7]), res[5], stack(res[3])
 
     spec_mat = P(("batch", "row"), "col", None)
     spec_out = (spec_mat, P("batch"), P("batch", None, None))

time: 221 us -> 218 us (0.986)
  transfers between devices with their start and end apart: 4 -> 4, of which waited for: 1 -> 1; matrix products, arithmetic and copies ran while one was open for 0% -> 1% of each run, Pallas kernels for 41% -> 42%
where the time goes in v3:
time: 218 us; the launch traced here: 214 us
  Pallas kernels  201 us (92%)
  starting transfers between devices  4.67 us (2%)
  local copies, waits for them, and re-layouts  3.58 us (2%)
    pallas_call x1, Pallas kernels, exchange(): pl.pallas_call(exchange_kernel, in_specs=[hbm, hbm], out_specs=[hbm] * 6...  112 us
    pallas_call x2, Pallas kernels, apply_update(): pl.pallas_call(body, grid=(steps,), in_specs=[blk2, pl.BlockSpec((own, nb...  89.4 us
  transfers between devices with their start and end apart: 4, of which 1 were waited for; matrix products, arithmetic and copies ran while one was open for 1% of the time, Pallas kernels for 42%

profile of v3, /device:TPU:0, one launch (start us, length us, event | category | flops | bytes accessed | tf_op | source)
XLA Modules:
  0.0 214.0 jit_solution(10045641141557120618)
XLA Ops:
  0.6 111.5 %shard_map.73 = (f32[128,4096]{1,0:T(8,128)}, f32[128,4096]{1,0:T(8,128)}, f32[2048,256]{1,0:T(8,128)}, f32[2048,256]{1,0:T(8,128)}, f32[1024,256]{1,0:T(8,128)}...) custom-call(f32[2048,4096]{1,0:T(8,128)} %bitcast.142, ...), custom_call_target="tpu_custom_call" | custom-call | flops 51539607552 | bytes 67108864 | tf_op jit(solution)/shard_map/pallas_call | solution.py:570
  112.1 0.9 collective-permute-start.9
  113.0 0.0 copy-start.1
  113.0 49.6 %shard_map.74 = (f32[2048,4096]{1,0:T(8,128)}, f32[8,128]{1,0:T(8,128)}, f32[256,256]{1,0:T(8,128)}, f32[256,256]{1,0:T(8,128)}, f32[128,256]{1,0:T(8,128)}, /*i...) custom-call(f32[2048,4096]{1,0:T(8,128)} %bitcast.143, ...), custom_call_target="tpu_custom_call" | custom-call | flops 25769803776 | bytes 67108864 | tf_op jit(solution)/shard_map/pallas_call | solution.py:657
  162.6 0.0 collective-permute-done.9
  162.6 0.0 copy-done.1
  162.6 0.1 add.292.p_ref
  162.8 0.0 copy-start.2
  162.8 0.0 collective-permute-start.10
  162.8 3.1 %collective-permute-start.8 = (f32[520,64]{1,0:T(8,128)}, f32[520,64]{1,0:T(8,128)S(1)}, u32[]{:S(2)}, u32[]{:S(2)}) collective-permute-start(f32[520,64]{1,0:T(8,128)} %get-tuple-element.1023), channel_id=1, source_target_pairs={{0,4},{1,5},{2,6},{3,7}} | collective-permute-start | bytes 399368 | tf_op jit(solution)/shard_map/ppermute | solution.py:773
  165.9 0.0 collective-permute-done.10.q_ref
  165.9 0.0 copy-start.6
  165.9 0.0 copy-done.2
  166.0 1.0 copy-done.6
  166.9 0.0 copy-start.3
  166.9 39.8 %shard_map.75 = (f32[2048,4096]{1,0:T(8,128)}, f32[8,128]{1,0:T(8,128)S(1)}) custom-call(f32[2048,4096]{1,0:T(8,128)} %bitcast.141, f32[128,4096]{1,0:T(8,128)} %get-tuple-element.1024.x_ref, f32[1024,256]{1,0:T(8,128)} %copy-done.2, f32[1024,256]{1,0:T(8,128)} %copy-done.6, f32[2048,256]{1,0:T(8,128)} %get-tuple-element.1028.c1_ref, ...), custom_call_target="tpu_custom_call" | custom-call | flops 25769803776 | bytes 67108864 | tf_op jit(solution)/shard_map/pallas_call | solution.py:657
  206.8 0.0 copy-start.4
  206.8 0.0 collective-permute-done.8
  206.8 0.0 copy-done.3
  206.8 0.7 fusion.44
  207.5 0.7 collective-permute-start.11
  208.2 0.6 reshape.163
  208.9 0.6 reshape.164
  209.5 1.6 collective-permute-done.11
  211.2 0.0 copy-start.5
  211.2 0.0 copy-done.4
  211.2 0.6 copy-done.5
  211.7 1.9 while.215
  211.7 1.3 add_reduce_fusion.1
  (2 shorter events, 0.0 us)
Async XLA Ops:
  112.1 50.5 %collective-permute-start.9 = (f32[1024,256]{1,0:T(8,128)}, f32[1024,256]{1,0:T(8,128)S(1)}, u32[]{:S(2)}, u32[]{:S(2)}) collective-permute-start(f32[1024,256]{1,0:T(8,128)} %get-tuple-element.1025), channel_id=1, source_target_pairs={{0,2},{2,0},{1,3},{3,1},{4,6},{6,4},{5,7},{7,5}} | collective-permute-start | bytes 3145736 | tf_op jit(solution)/shard_map/ppermute | solution.py:768
  113.0 49.6 %copy-start.1 = (f32[1024,256]{1,0:T(8,128)S(1)}, f32[1024,256]{1,0:T(8,128)}, u32[]{:S(2)}) copy-start(f32[1024,256]{1,0:T(8,128)} %get-tuple-element.1025) | copy-start | bytes 3145732
  162.8 3.2 %copy-start.2 = (f32[1024,256]{1,0:T(8,128)}, f32[1024,256]{1,0:T(8,128)S(1)}, u32[]{:S(2)}) copy-start(f32[1024,256]{1,0:T(8,128)S(1)} %add.292.p_ref) | copy-start | bytes 3145732
  162.8 3.1 %collective-permute-start.10 = (f32[1024,256]{1,0:T(8,128)S(1)}, f32[1024,256]{1,0:T(8,128)S(1)}, u32[]{:S(2)}, u32[]{:S(2)}) collective-permute-start(f32[1024,256]{1,0:T(8,128)S(1)} %add.292.p_ref), channel_id=1, source_target_pairs={{0,1},{1,0},{2,3},{3,2},{4,5},{5,4},{6,7},{7,6}} | collective-permute-start | bytes 3145736 | tf_op jit(solution)/shard_map/ppermute | solution.py:772
  162.8 43.9 %collective-permute-start.8 = (f32[520,64]{1,0:T(8,128)}, f32[520,64]{1,0:T(8,128)S(1)}, u32[]{:S(2)}, u32[]{:S(2)}) collective-permute-start(f32[520,64]{1,0:T(8,128)} %get-tuple-element.1023), channel_id=1, source_target_pairs={{0,4},{1,5},{2,6},{3,7}} | collective-permute-start | bytes 399368 | tf_op jit(solution)/shard_map/ppermute | solution.py:773
  165.9 1.0 copy-start.6
  166.9 39.8 %copy-start.3 = (f32[520,64]{1,0:T(8,128)S(1)}, f32[520,64]{1,0:T(8,128)}, u32[]{:S(2)}) copy-start(f32[520,64]{1,0:T(8,128)} %get-tuple-element.1023) | copy-start | bytes 399364
  206.8 4.4 %copy-start.4 = (f32[8,128]{1,0:T(8,128)}, f32[8,128]{1,0:T(8,128)S(1)}, u32[]{:S(2)}) copy-start(f32[8,128]{1,0:T(8,128)S(1)} %get-tuple-element.1915) | copy-start | bytes 12292
  207.5 3.6 %collective-permute-start.11 = (f32[8,128]{1,0:T(8,128)S(1)}, f32[8,128]{1,0:T(8,128)S(1)}, u32[]{:S(2)}, u32[]{:S(2)}) collective-permute-start(f32[8,128]{1,0:T(8,128)S(1)} %get-tuple-element.1915), channel_id=1, source_target_pairs={{0,4},{4,0},{1,5},{5,1},{2,6},{6,2},{3,7},{7,3}} | collective-permute-start | bytes 12296 | tf_op jit(solution)/shard_map/ppermute | solution.py:781
  211.2 0.6 copy-start.5

commit v4 on v3

--- a/solution.py
+++ b/solution.py
@@ -576,7 +576,7 @@
         + [pltpu.VMEM(s, F32) for s in after]
         + [dma(n) for n in ((SLOTS,), (4,), (4,), (ny,), (ny,), (6, 3), (6,), (2,), (2,), (6,), (6,), (2,), (2,), (2,), (2,))],
         cost_estimate=pl.CostEstimate(flops=24 * cols * rows * N, bytes_accessed=8 * cols * rows, transcendentals=0),
-        compiler_params=pltpu.CompilerParams(vmem_limit_bytes=60 * 2**20, collective_id=0, has_side_effects=True))(ca, cb)
+        compiler_params=pltpu.CompilerParams(vmem_limit_bytes=46 * 2**20, collective_id=0, has_side_effects=True))(ca, cb)
 
 
 def apply_update(ct, peer, psum, poth, c1, small, before, nxt=None, past=()):
@@ -661,7 +661,7 @@
         scratch_shapes=[pltpu.VMEM(s, F32) for s in scratch],
         out_shape=[jax.ShapeDtypeStruct(s, F32) for s in [(cols, rows), TILE] + more],
         cost_estimate=pl.CostEstimate(flops=12 * cols * rows * N, bytes_accessed=8 * cols * rows, transcendentals=0),
-        compiler_params=pltpu.CompilerParams(vmem_limit_bytes=60 * 2**20))(ct, peer, *consts)
+        compiler_params=pltpu.CompilerParams(vmem_limit_bytes=40 * 2**20))(ct, peer, *consts)
 
 
 R1 = [(0, 1), (1, 0), (2, 3), (3, 2)]
@@ -765,6 +765,7 @@
         cts = [m.transpose(1, 2, 0).reshape(cols, local_rows) for m in (a_matrix, b_matrix)]
 
         pa, pb, c1a, c1b, pam, pao, pbm, g, x1, *first = exchange(*cts, own)
+        c1a, c1b, pb = (pltpu.with_memory_space_constraint(x, pltpu.HBM) for x in (c1a, c1b, pb))
         across = lax.ppermute(pbm, "row", R2)
         out_a, bad_a, *second = apply_update(cts[0], pa, pam, pao, c1a, first, first[6], (g, x1), (first[4], first[5]))
         across, bad_a = lax.optimization_barrier((across, bad_a))

time: 218 us -> 213 us (0.977)
  Pallas kernels: 201 us -> 197 us
where the time goes in v4:
time: 213 us; the launch traced here: 210 us
  Pallas kernels  197 us (92%)
  starting transfers between devices  4.65 us (2%)
  local copies, waits for them, and re-layouts  2.59 us (1%)
    pallas_call x1, Pallas kernels, exchange(): pl.pallas_call(exchange_kernel, in_specs=[hbm, hbm], out_specs=[hbm] * 6...  110 us
    pallas_call x2, Pallas kernels, apply_update(): pl.pallas_call(body, grid=(steps,), in_specs=[blk2, pl.BlockSpec((own, nb...  87.7 us
  transfers between devices with their start and end apart: 4, of which 1 were waited for; matrix products, arithmetic and copies ran while one was open for 1% of the time, Pallas kernels for 42%

profile of v4, /device:TPU:0, one launch (start us, length us, event | category | flops | bytes accessed | tf_op | source)
XLA Modules:
  0.0 209.6 jit_solution(630525213064785392)
XLA Ops:
  0.6 109.8 %shard_map.73 = (f32[128,4096]{1,0:T(8,128)S(1)}, f32[128,4096]{1,0:T(8,128)}, f32[2048,256]{1,0:T(8,128)}, f32[2048,256]{1,0:T(8,128)}, f32[1024,256]{1,0:T(8,1...) custom-call(f32[2048,4096]{1,0:T(8,128)} %bitcast.142, ...), custom_call_target="tpu_custom_call" | custom-call | flops 51539607552 | bytes 67108864 | tf_op jit(solution)/shard_map/pallas_call | solution.py:570
  110.5 0.7 collective-permute-start.9
  111.2 47.3 %shard_map.74 = (f32[2048,4096]{1,0:T(8,128)}, f32[8,128]{1,0:T(8,128)S(1)}, f32[256,256]{1,0:T(8,128)S(1)}, f32[256,256]{1,0:T(8,128)S(1)}, f32[128,256]{1,0:T(...) custom-call(f32[2048,4096]{1,0:T(8,128)} %bitcast.143, ...), custom_call_target="tpu_custom_call" | custom-call | flops 25769803776 | bytes 67108864 | tf_op jit(solution)/shard_map/pallas_call | solution.py:657
  158.5 0.0 collective-permute-done.9
  158.5 0.1 add.292.p_ref
  158.6 0.0 collective-permute-start.10
  158.7 3.3 %collective-permute-start.8 = (f32[520,64]{1,0:T(8,128)S(1)}, f32[520,64]{1,0:T(8,128)S(1)}, u32[]{:S(2)}, u32[]{:S(2)}) collective-permute-start(f32[520,64]{1,0:T(8,128)S(1)} %get-tuple-element.1023), channel_id=1, source_target_pairs={{0,4},{1,5},{2,6},{3,7}} | collective-permute-start | bytes 399368 | tf_op jit(solution)/shard_map/ppermute | solution.py:774
  161.9 0.0 collective-permute-done.10.q_ref
  161.9 40.4 %shard_map.75 = (f32[2048,4096]{1,0:T(8,128)}, f32[8,128]{1,0:T(8,128)S(1)}) custom-call(f32[2048,4096]{1,0:T(8,128)} %bitcast.141, f32[128,4096]{1,0:T(8,128)} %get-tuple-element.1024.x_ref, f32[1024,256]{1,0:T(8,128)S(1)} %add.292.p_ref, f32[1024,256]{1,0:T(8,128)S(1)} %collective-permute-done.10.q_ref, f32[2048,256]{1,0:T(8,128)} %get-tuple-element.1028.c1_ref, ...), custom_call_target="tpu_custom_call" | custom-call | flops 25769803776 | bytes 67108864 | tf_op jit(solution)/shard_map/pallas_call | solution.py:657
  202.3 0.0 copy-start.1
  202.3 0.0 collective-permute-done.8
  202.4 0.7 fusion.44
  203.1 0.7 collective-permute-start.11
  203.8 0.6 reshape.163
  204.4 0.6 reshape.164
  205.0 1.6 collective-permute-done.11
  206.7 0.0 copy-start.2
  206.7 0.0 copy-done.1
  206.7 0.6 copy-done.2
  207.3 1.9 while.215
  207.3 1.3 add_reduce_fusion.1
  (2 shorter events, 0.0 us)
Async XLA Ops:
  110.5 48.0 %collective-permute-start.9 = (f32[1024,256]{1,0:T(8,128)S(1)}, f32[1024,256]{1,0:T(8,128)S(1)}, u32[]{:S(2)}, u32[]{:S(2)}) collective-permute-start(f32[1024,256]{1,0:T(8,128)S(1)} %get-tuple-element.1025), channel_id=1, source_target_pairs={{0,2},{2,0},{1,3},{3,1},{4,6},{6,4},{5,7},{7,5}} | collective-permute-start | bytes 3145736 | tf_op jit(solution)/shard_map/ppermute | solution.py:769
  158.6 3.3 %collective-permute-start.10 = (f32[1024,256]{1,0:T(8,128)S(1)}, f32[1024,256]{1,0:T(8,128)S(1)}, u32[]{:S(2)}, u32[]{:S(2)}) collective-permute-start(f32[1024,256]{1,0:T(8,128)S(1)} %add.292.p_ref), channel_id=1, source_target_pairs={{0,1},{1,0},{2,3},{3,2},{4,5},{5,4},{6,7},{7,6}} | collective-permute-start | bytes 3145736 | tf_op jit(solution)/shard_map/ppermute | solution.py:773
  158.7 43.7 %collective-permute-start.8 = (f32[520,64]{1,0:T(8,128)S(1)}, f32[520,64]{1,0:T(8,128)S(1)}, u32[]{:S(2)}, u32[]{:S(2)}) collective-permute-start(f32[520,64]{1,0:T(8,128)S(1)} %get-tuple-element.1023), channel_id=1, source_target_pairs={{0,4},{1,5},{2,6},{3,7}} | collective-permute-start | bytes 399368 | tf_op jit(solution)/shard_map/ppermute | solution.py:774
  202.3 4.4 %copy-start.1 = (f32[8,128]{1,0:T(8,128)}, f32[8,128]{1,0:T(8,128)S(1)}, u32[]{:S(2)}) copy-start(f32[8,128]{1,0:T(8,128)S(1)} %get-tuple-element.1915) | copy-start | bytes 12292
  203.1 3.6 %collective-permute-start.11 = (f32[8,128]{1,0:T(8,128)S(1)}, f32[8,128]{1,0:T(8,128)S(1)}, u32[]{:S(2)}, u32[]{:S(2)}) collective-permute-start(f32[8,128]{1,0:T(8,128)S(1)} %get-tuple-element.1915), channel_id=1, source_target_pairs={{0,4},{4,0},{1,5},{5,1},{2,6},{6,2},{3,7},{7,3}} | collective-permute-start | bytes 12296 | tf_op jit(solution)/shard_map/ppermute | solution.py:782
  206.7 0.6 copy-start.2

commit v5 on v4

--- a/solution.py
+++ b/solution.py
@@ -37,12 +37,11 @@
     return lax.dot_general(a, b, dn, precision=HI, preferred_element_type=F32)
 
 
-GROUP = 4
 AMPLIFY = 64.0
 HUGE = 1e9
 
 
-def diag_factor(mats):
+def diag_factor(mats, group):
     tiles = W // 8
     lane8 = lanes_of(TILE)
     sub8 = rows_of(TILE)
@@ -57,12 +56,12 @@
         yw = jnp.concatenate([ypp, eye], 1)
         st.append(dict(he=[he[8 * g:8 * g + 8] for g in range(tiles)], yw=[yw[8 * g:8 * g + 8] for g in range(tiles)],
                        l=[zeros] * tiles, u=[zeros] * tiles, tau=zeros))
-    for k0 in range(0, W, GROUP):
+    for k0 in range(0, W, group):
         gk = k0 // 8
         for s in st:
-            s['bh'] = [[full(s['he'][g][:, k:k + 1]) for g in range(gk, tiles)] for k in range(k0, k0 + GROUP)]
-            s['by'] = [[full(s['yw'][g][:, k:k + 1]) for g in range(tiles)] for k in range(k0, k0 + GROUP)]
-        for k in range(k0, k0 + GROUP):
+            s['bh'] = [[full(s['he'][g][:, k:k + 1]) for g in range(gk, tiles)] for k in range(k0, k0 + group)]
+            s['by'] = [[full(s['yw'][g][:, k:k + 1]) for g in range(tiles)] for k in range(k0, k0 + group)]
+        for k in range(k0, k0 + group):
             sk = k - 8 * gk
             isk = sub8 == sk
             for s in st:
@@ -78,7 +77,7 @@
                 u = pick(s['yw'][gk]) - jnp.where((lane8 >= k) & (lane8 < W), r, 0.0)
                 un = u * uinv
                 rr = r * rinv
-                for k2 in range(k + 1, k0 + GROUP):
+                for k2 in range(k + 1, k0 + group):
                     r2 = pick(s['bh'][k2 - k0][0]) * rinv
                     un2 = (pick(s['by'][k2 - k0][gk]) - r2) * uinv
                     rr2 = r2 * rinv
@@ -144,9 +143,9 @@
     norm[...] = jnp.broadcast_to(jnp.sqrt(total(dg, 0)), (8, N))
 
 
-def chain_cols(p, st):
+def chain_cols(p, st, group):
     hs, ys, _, fac, _, tv = st
-    e, l, u, w, tau = diag_factor([(hs[0:W, 0:W], ys[0:W, 0:W])])[0]
+    e, l, u, w, tau = diag_factor([(hs[0:W, 0:W], ys[0:W, 0:W])], group)[0]
     for i, x in enumerate((e, l, u, w)):
         fac[p, i] = x
     tv[pl.ds(p, 1), :] = tau
@@ -476,7 +475,7 @@
 
                     @pl.when(live)
                     def _():
-                        chain_cols(t - begin, st)
+                        chain_cols(t - begin, st, 8)
                         run()
                         weave(chain_update(t - begin, st), [])
 
@@ -631,7 +630,7 @@
         else:
             @pl.when(lax.rem(i, 2) == 0)
             def _():
-                chain_cols(lax.div(i, 2), st)
+                chain_cols(lax.div(i, 2), st, 4)
                 weave([], pieces)
 
             @pl.when(lax.rem(i, 2) == 1)
@@ -771,7 +770,7 @@
         across, bad_a = lax.optimization_barrier((across, bad_a))
         pbm = pbm + across
         pbo = lax.ppermute(pbm, "row", R1)
-        small = lax.ppermute(second[4], "col", [(0, 1)])
+        small = lax.ppermute(second[4], "col", CY)
         out_b, bad = apply_update(cts[1], pb, pbm, pbo, c1b, second, bad_a)
         small, bad = lax.optimization_barrier((small, bad))
         tt = jnp.where(col_rank == 0, second[4], small)

time: 213 us -> 211 us (level)
  transfers between devices with their start and end apart: 4 -> 4, of which waited for: 1 -> 2; matrix products, arithmetic and copies ran while one was open for 1% -> 1% of each run, Pallas kernels for 42% -> 42%
where the time goes in v5:
time: 211 us; the launch traced here: 208 us
  Pallas kernels  197 us (93%)
  starting transfers between devices  3.61 us (2%)
  local copies, waits for them, and re-layouts  2.59 us (1%)
    pallas_call x1, Pallas kernels, exchange(): pl.pallas_call(exchange_kernel, in_specs=[hbm, hbm], out_specs=[hbm] * 6...  109 us
    pallas_call x2, Pallas kernels, apply_update(): pl.pallas_call(body, grid=(steps,), in_specs=[blk2, pl.BlockSpec((own, nb...  87.6 us
  transfers between devices with their start and end apart: 4, of which 2 were waited for; matrix products, arithmetic and copies ran while one was open for 1% of the time, Pallas kernels for 42%

profile of v5, /device:TPU:0, one launch (start us, length us, event | category | flops | bytes accessed | tf_op | source)
XLA Modules:
  0.0 207.9 jit_solution(6268692535512695779)
XLA Ops:
  0.6 108.9 %shard_map.73 = (f32[128,4096]{1,0:T(8,128)S(1)}, f32[128,4096]{1,0:T(8,128)}, f32[2048,256]{1,0:T(8,128)}, f32[2048,256]{1,0:T(8,128)}, f32[1024,256]{1,0:T(8,1...) custom-call(f32[2048,4096]{1,0:T(8,128)} %bitcast.142, ...), custom_call_target="tpu_custom_call" | custom-call | flops 51539607552 | bytes 67108864 | tf_op jit(solution)/shard_map/pallas_call | solution.py:569
  109.6 0.6 collective-permute-start.9
  110.2 47.3 %shard_map.74 = (f32[2048,4096]{1,0:T(8,128)}, f32[8,128]{1,0:T(8,128)S(1)}, f32[256,256]{1,0:T(8,128)S(1)}, f32[256,256]{1,0:T(8,128)S(1)}, f32[128,256]{1,0:T(...) custom-call(f32[2048,4096]{1,0:T(8,128)} %bitcast.143, ...), custom_call_target="tpu_custom_call" | custom-call | flops 25769803776 | bytes 67108864 | tf_op jit(solution)/shard_map/pallas_call | solution.py:656
  157.5 0.0 collective-permute-done.9
  157.5 0.1 add.292.p_ref
  157.6 0.0 collective-permute-start.10
  157.6 1.5 collective-permute-start.8
  159.2 1.1 collective-permute-done.10.q_ref
  160.3 40.3 %shard_map.75 = (f32[2048,4096]{1,0:T(8,128)}, f32[8,128]{1,0:T(8,128)S(1)}) custom-call(f32[2048,4096]{1,0:T(8,128)} %bitcast.141, f32[128,4096]{1,0:T(8,128)} %get-tuple-element.1024.x_ref, f32[1024,256]{1,0:T(8,128)S(1)} %add.292.p_ref, f32[1024,256]{1,0:T(8,128)S(1)} %collective-permute-done.10.q_ref, f32[2048,256]{1,0:T(8,128)} %get-tuple-element.1028.c1_ref, ...), custom_call_target="tpu_custom_call" | custom-call | flops 25769803776 | bytes 67108864 | tf_op jit(solution)/shard_map/pallas_call | solution.py:656
  200.6 0.0 copy-start.1
  200.6 0.0 collective-permute-done.8
  200.7 0.7 fusion.44
  201.4 1.5 collective-permute-start.11
  202.9 0.6 reshape.163
  203.5 0.6 reshape.164
  204.2 0.8 collective-permute-done.11
  205.0 0.0 copy-start.2
  205.0 0.0 copy-done.1
  205.0 0.6 copy-done.2
  205.6 1.9 while.215
  205.6 1.3 add_reduce_fusion.1
  (2 shorter events, 0.0 us)
Async XLA Ops:
  109.6 47.9 %collective-permute-start.9 = (f32[1024,256]{1,0:T(8,128)S(1)}, f32[1024,256]{1,0:T(8,128)S(1)}, u32[]{:S(2)}, u32[]{:S(2)}) collective-permute-start(f32[1024,256]{1,0:T(8,128)S(1)} %get-tuple-element.1025), channel_id=1, source_target_pairs={{0,2},{2,0},{1,3},{3,1},{4,6},{6,4},{5,7},{7,5}} | collective-permute-start | bytes 3145736 | tf_op jit(solution)/shard_map/ppermute | solution.py:768
  157.6 2.7 %collective-permute-start.10 = (f32[1024,256]{1,0:T(8,128)S(1)}, f32[1024,256]{1,0:T(8,128)S(1)}, u32[]{:S(2)}, u32[]{:S(2)}) collective-permute-start(f32[1024,256]{1,0:T(8,128)S(1)} %add.292.p_ref), channel_id=1, source_target_pairs={{0,1},{1,0},{2,3},{3,2},{4,5},{5,4},{6,7},{7,6}} | collective-permute-start | bytes 3145736 | tf_op jit(solution)/shard_map/ppermute | solution.py:772
  157.6 43.0 %collective-permute-start.8 = (f32[520,64]{1,0:T(8,128)S(1)}, f32[520,64]{1,0:T(8,128)S(1)}, u32[]{:S(2)}, u32[]{:S(2)}) collective-permute-start(f32[520,64]{1,0:T(8,128)S(1)} %get-tuple-element.1023), channel_id=1, source_target_pairs={{0,4},{4,0},{1,5},{5,1},{2,6},{6,2},{3,7},{7,3}} | collective-permute-start | bytes 399368 | tf_op jit(solution)/shard_map/ppermute | solution.py:773
  200.6 4.4 %copy-start.1 = (f32[8,128]{1,0:T(8,128)}, f32[8,128]{1,0:T(8,128)S(1)}, u32[]{:S(2)}) copy-start(f32[8,128]{1,0:T(8,128)S(1)} %get-tuple-element.1915) | copy-start | bytes 12292
  201.4 3.6 %collective-permute-start.11 = (f32[8,128]{1,0:T(8,128)S(1)}, f32[8,128]{1,0:T(8,128)S(1)}, u32[]{:S(2)}, u32[]{:S(2)}) collective-permute-start(f32[8,128]{1,0:T(8,128)S(1)} %get-tuple-element.1915), channel_id=1, source_target_pairs={{0,4},{4,0},{1,5},{5,1},{2,6},{6,2},{3,7},{7,3}} | collective-permute-start | bytes 12296 | tf_op jit(solution)/shard_map/ppermute | solution.py:781
  205.0 0.6 copy-start.2

commit v6 on v5

--- a/solution.py
+++ b/solution.py
@@ -311,8 +311,6 @@
     for t in range(AHEAD):
         c_copy(0, t).start()
 
-    for m in BOTH:
-        acc[m, 0:nown, :] = jnp.zeros((nown, N), F32)
     barrier = pltpu.get_barrier_semaphore()
     for where in (dict(row=mate), dict(row=across), dict(row=diag), dict(col=1 - col)):
         pl.semaphore_signal(barrier, device_id=where, device_id_type=pl.DeviceIdType.MESH)
@@ -418,10 +416,12 @@
             s = pl.ds(pl.multiple_of(q * HALF, HALF), HALF)
             for i, part in enumerate(split3(own[m, :, s])):
                 xo[m, i, :, s] = part
+            acc[m, pl.ds(pl.multiple_of(q * N, N), N), :] = jnp.zeros((N, N), F32)
             return 0
 
         own_copies[m].wait()
-        loop(rows // HALF, build, 0)
+        gacc[m] = jnp.zeros((N, N), F32)
+        loop(cols // N, build, 0)
 
     def panel(m, s0, width):
         return [jnp.concatenate([xo[m, i, :, pl.ds(s0, width)], xs[i, :, 0:width]], 0) for i in SPLITS]
@@ -434,19 +434,19 @@
         x = panel(m, s0, width)
         return dot6(x, x, NT)
 
-    def trip(m, j, slot, s0, width, fresh):
+    def trip(m, j, slot, s0, width):
         x = panel(m, s0, width)
         for i in range(CHUNK // PIECE):
             r = dot6(split3(cbuf[slot, i * PIECE:(i + 1) * PIECE, 0:width]), x, NT)
             d = pl.ds(pl.multiple_of(nown + j * CHUNK + i * PIECE, 32), PIECE)
-            acc[m, d, :] = jnp.where(fresh, r, acc[m, d, :] + r)
+            acc[m, d, :] = acc[m, d, :] + r
 
     def products(m, count):
         def span(h, _):
             y_copy(m, h).wait_recv()
             s0 = pl.multiple_of(h * SPAN, SPAN)
             r = head(m, s0, SPAN)
-            gacc[m] = jnp.where(h == 0, r, gacc[m] + r)
+            gacc[m] = gacc[m] + r
 
             if m == 0:
                 @pl.when(h == spans - 1)
@@ -467,7 +467,7 @@
                 def _():
                     (c_copy(1, ahead) if m == 0 else c_half(ahead)).start()
 
-                run = functools.partial(trip, m, j, slot, s0, SPAN, h == 0)
+                run = functools.partial(trip, m, j, slot, s0, SPAN)
                 if m == 0:
                     run()
                 else:
@@ -507,7 +507,7 @@
                 def _():
                     c_half(u + AHEAD).start()
 
-                trip(1, j, half_slot(u), s0, HALF, False)
+                trip(1, j, half_slot(u), s0, HALF)
 
                 @pl.when(u == nchunk)
                 def _():

time: 211 us -> 211 us (level)
  no operation moved by 1% of the time
where the time goes in v6:
time: 211 us; the launch traced here: 208 us
  Pallas kernels  197 us (93%)
  starting transfers between devices  3.54 us (2%)
  local copies, waits for them, and re-layouts  2.59 us (1%)
    pallas_call x1, Pallas kernels, exchange(): pl.pallas_call(exchange_kernel, in_specs=[hbm, hbm], out_specs=[hbm] * 6...  109 us
    pallas_call x2, Pallas kernels, apply_update(): pl.pallas_call(body, grid=(steps,), in_specs=[blk2, pl.BlockSpec((own, nb...  87.6 us
  transfers between devices with their start and end apart: 4, of which 2 were waited for; matrix products, arithmetic and copies ran while one was open for 1% of the time, Pallas kernels for 42%

profile of v6, /device:TPU:0, one launch (start us, length us, event | category | flops | bytes accessed | tf_op | source)
XLA Modules:
  0.0 207.9 jit_solution(8868105436562067542)
XLA Ops:
  0.6 108.9 %shard_map.73 = (f32[128,4096]{1,0:T(8,128)S(1)}, f32[128,4096]{1,0:T(8,128)}, f32[2048,256]{1,0:T(8,128)}, f32[2048,256]{1,0:T(8,128)}, f32[1024,256]{1,0:T(8,1...) custom-call(f32[2048,4096]{1,0:T(8,128)} %bitcast.142, ...), custom_call_target="tpu_custom_call" | custom-call | flops 51539607552 | bytes 67108864 | tf_op jit(solution)/shard_map/pallas_call | solution.py:569
  109.5 0.6 collective-permute-start.9
  110.1 47.3 %shard_map.74 = (f32[2048,4096]{1,0:T(8,128)}, f32[8,128]{1,0:T(8,128)S(1)}, f32[256,256]{1,0:T(8,128)S(1)}, f32[256,256]{1,0:T(8,128)S(1)}, f32[128,256]{1,0:T(...) custom-call(f32[2048,4096]{1,0:T(8,128)} %bitcast.143, ...), custom_call_target="tpu_custom_call" | custom-call | flops 25769803776 | bytes 67108864 | tf_op jit(solution)/shard_map/pallas_call | solution.py:656
  157.4 0.0 collective-permute-done.9
  157.4 0.1 add.292.p_ref
  157.5 0.0 collective-permute-start.10
  157.6 1.5 collective-permute-start.8
  159.1 1.2 collective-permute-done.10.q_ref
  160.2 40.3 %shard_map.75 = (f32[2048,4096]{1,0:T(8,128)}, f32[8,128]{1,0:T(8,128)S(1)}) custom-call(f32[2048,4096]{1,0:T(8,128)} %bitcast.141, f32[128,4096]{1,0:T(8,128)} %get-tuple-element.1024.x_ref, f32[1024,256]{1,0:T(8,128)S(1)} %add.292.p_ref, f32[1024,256]{1,0:T(8,128)S(1)} %collective-permute-done.10.q_ref, f32[2048,256]{1,0:T(8,128)} %get-tuple-element.1028.c1_ref, ...), custom_call_target="tpu_custom_call" | custom-call | flops 25769803776 | bytes 67108864 | tf_op jit(solution)/shard_map/pallas_call | solution.py:656
  200.6 0.0 copy-start.1
  200.6 0.0 collective-permute-done.8
  200.6 0.7 fusion.44
  201.3 1.5 collective-permute-start.11
  202.8 0.6 reshape.163
  203.4 0.6 reshape.164
  204.1 0.9 collective-permute-done.11
  204.9 0.0 copy-start.2
  204.9 0.0 copy-done.1
  205.0 0.6 copy-done.2
  205.5 1.9 while.215
  205.5 1.3 add_reduce_fusion.1
  (2 shorter events, 0.0 us)
Async XLA Ops:
  109.5 47.9 %collective-permute-start.9 = (f32[1024,256]{1,0:T(8,128)S(1)}, f32[1024,256]{1,0:T(8,128)S(1)}, u32[]{:S(2)}, u32[]{:S(2)}) collective-permute-start(f32[1024,256]{1,0:T(8,128)S(1)} %get-tuple-element.1025), channel_id=1, source_target_pairs={{0,2},{2,0},{1,3},{3,1},{4,6},{6,4},{5,7},{7,5}} | collective-permute-start | bytes 3145736 | tf_op jit(solution)/shard_map/ppermute | solution.py:768
  157.5 2.7 %collective-permute-start.10 = (f32[1024,256]{1,0:T(8,128)S(1)}, f32[1024,256]{1,0:T(8,128)S(1)}, u32[]{:S(2)}, u32[]{:S(2)}) collective-permute-start(f32[1024,256]{1,0:T(8,128)S(1)} %add.292.p_ref), channel_id=1, source_target_pairs={{0,1},{1,0},{2,3},{3,2},{4,5},{5,4},{6,7},{7,6}} | collective-permute-start | bytes 3145736 | tf_op jit(solution)/shard_map/ppermute | solution.py:772
  157.6 43.0 %collective-permute-start.8 = (f32[520,64]{1,0:T(8,128)S(1)}, f32[520,64]{1,0:T(8,128)S(1)}, u32[]{:S(2)}, u32[]{:S(2)}) collective-permute-start(f32[520,64]{1,0:T(8,128)S(1)} %get-tuple-element.1023), channel_id=1, source_target_pairs={{0,4},{4,0},{1,5},{5,1},{2,6},{6,2},{3,7},{7,3}} | collective-permute-start | bytes 399368 | tf_op jit(solution)/shard_map/ppermute | solution.py:773
  200.6 4.4 %copy-start.1 = (f32[8,128]{1,0:T(8,128)}, f32[8,128]{1,0:T(8,128)S(1)}, u32[]{:S(2)}) copy-start(f32[8,128]{1,0:T(8,128)S(1)} %get-tuple-element.1915) | copy-start | bytes 12292
  201.3 3.6 %collective-permute-start.11 = (f32[8,128]{1,0:T(8,128)S(1)}, f32[8,128]{1,0:T(8,128)S(1)}, u32[]{:S(2)}, u32[]{:S(2)}) collective-permute-start(f32[8,128]{1,0:T(8,128)S(1)} %get-tuple-element.1915), channel_id=1, source_target_pairs={{0,4},{4,0},{1,5},{5,1},{2,6},{6,2},{3,7},{7,3}} | collective-permute-start | bytes 12296 | tf_op jit(solution)/shard_map/ppermute | solution.py:781
  204.9 0.6 copy-start.2
